TPU v7x, 8 devices: a whole 2x2x1 slice. The times are simulated.
8 devices in a mesh: pool: 8 (over z, y, x, core).
Axes of the slice: x: 2, y: 2, z: 1, core: 2. Of those that a mesh axis runs over, the one named last changes fastest.
Arguments:
- hidden: bfloat16 [8, 64, 2048], P('pool')
- prefix_len: int32 [8], P('pool')
- prefix_table: int32 [8, 256, 2], P('pool')
- write_table: int32 [8, 1, 2], P('pool')
- cache_c: bfloat16 [8, 5, 64, 512], P('pool')
- cache_kr: bfloat16 [8, 5, 64, 64], P('pool')
- w_q: bfloat16 [2048, 3072], replicated
- w_dkv: bfloat16 [2048, 576], replicated
- g_kv: bfloat16 [512], replicated
- w_uk: bfloat16 [512, 16, 128], replicated
- w_uv: bfloat16 [512, 16, 128], replicated
- w_o: bfloat16 [2048, 2048], replicated
Outputs:
- output 1: bfloat16 [8, 64, 2048], P('pool')
- output 2: bfloat16 [8, 5, 64, 512], P('pool')
- output 3: bfloat16 [8, 5, 64, 64], P('pool')
All inputs are finite; a program needn't handle non-finite values.
Results may differ from a plain program's by a relative error of at most 0.00713187.
Values are sent between devices in bfloat16 or wider.
A program may use at most 1 GiB of HBM per device.

v0:
```python
import jax
import jax.numpy as jnp
from jax import lax
from jax.sharding import PartitionSpec as P

PAGE_LEN = 64
LATENT = 512
ROPE_DIM = 64
NOPE_DIM = 128
NORM_EPS = 1e-6
ROPE_BASE = 10000.0


def rope_tables(positions):
    half_dim = ROPE_DIM // 2
    inv_freq = ROPE_BASE ** (-jnp.arange(half_dim, dtype=jnp.float32) / half_dim)
    angles = positions.astype(jnp.float32)[..., None] * inv_freq
    return jnp.cos(angles), jnp.sin(angles)


def apply_rope(values, cos_tab, sin_tab):
    half_dim = ROPE_DIM // 2
    first = values[..., :half_dim]
    second = values[..., half_dim:]
    return jnp.concatenate([first * cos_tab - second * sin_tab, second * cos_tab + first * sin_tab], axis=-1)


def chunk_project(hidden, pre_len, w_q, w_dkv, g_kv, w_uk):
    req_count, chunk_len, d_model = hidden.shape
    head_count = w_uk.shape[1]
    x_rows = hidden.reshape(req_count * chunk_len, d_model)
    q_all = jnp.dot(x_rows, w_q, preferred_element_type=jnp.float32).astype(jnp.bfloat16)
    q_all = q_all.reshape(req_count, chunk_len, head_count, NOPE_DIM + ROPE_DIM)
    kv_lat = jnp.dot(x_rows, w_dkv, preferred_element_type=jnp.float32).reshape(req_count, chunk_len, LATENT + ROPE_DIM)
    lat_part = kv_lat[..., :LATENT]
    inv_rms = lax.rsqrt(jnp.mean(lat_part * lat_part, axis=-1, keepdims=True) + NORM_EPS)
    c_new = (lat_part * inv_rms * g_kv.astype(jnp.float32)).astype(jnp.bfloat16)
    cos_tab, sin_tab = rope_tables(pre_len[:, None] + jnp.arange(chunk_len)[None, :])
    kr_new = apply_rope(kv_lat[..., LATENT:], cos_tab, sin_tab).astype(jnp.bfloat16)
    q_rope = apply_rope(q_all[..., NOPE_DIM:].astype(jnp.float32), cos_tab[:, :, None, :], sin_tab[:, :, None, :]).astype(jnp.bfloat16)
    q_lat = jnp.einsum("rchn,lhn->rchl", q_all[..., :NOPE_DIM], w_uk, preferred_element_type=jnp.float32).astype(jnp.bfloat16)
    return jnp.concatenate([q_lat, q_rope], axis=-1), jnp.concatenate([c_new, kr_new], axis=-1)


def finish(o_lat, hidden, w_uv, w_o):
    req_count, chunk_len, d_model = hidden.shape
    o_heads = jnp.einsum("rhcl,lhv->rchv", o_lat, w_uv, preferred_element_type=jnp.float32).astype(jnp.bfloat16)
    attn_out = jnp.dot(o_heads.reshape(req_count * chunk_len, -1), w_o, preferred_element_type=jnp.float32)
    y_rows = hidden.reshape(req_count * chunk_len, d_model).astype(jnp.float32) + attn_out
    return y_rows.astype(jnp.bfloat16).reshape(req_count, chunk_len, d_model)


def attend(q_cat, new_keys, prefix_keys, pre_len, hidden, w_uv, w_o):
    chunk_len = q_cat.shape[1]
    prefix_max = prefix_keys.shape[1]
    score_scale = (NOPE_DIM + ROPE_DIM) ** -0.5
    s_pre = jnp.einsum("rchk,rjk->rhcj", q_cat, prefix_keys, preferred_element_type=jnp.float32) * score_scale
    s_new = jnp.einsum("rchk,rjk->rhcj", q_cat, new_keys, preferred_element_type=jnp.float32) * score_scale
    pre_mask = (jnp.arange(prefix_max)[None, :] < pre_len[:, None])[:, None, None, :]
    causal = jnp.arange(chunk_len)[None, :] <= jnp.arange(chunk_len)[:, None]
    s_pre = jnp.where(pre_mask, s_pre, -jnp.inf)
    s_new = jnp.where(causal, s_new, -jnp.inf)
    row_max = jnp.maximum(jnp.max(s_pre, axis=-1, keepdims=True), jnp.max(s_new, axis=-1, keepdims=True))
    e_pre = jnp.exp(s_pre - row_max)
    e_new = jnp.exp(s_new - row_max)
    denom_sum = jnp.sum(e_pre, axis=-1, keepdims=True) + jnp.sum(e_new, axis=-1, keepdims=True)
    o_lat = jnp.einsum("rhcj,rjl->rhcl", (e_pre / denom_sum).astype(jnp.bfloat16), prefix_keys[..., :LATENT], preferred_element_type=jnp.float32)
    o_lat = o_lat + jnp.einsum("rhcj,rjl->rhcl", (e_new / denom_sum).astype(jnp.bfloat16), new_keys[..., :LATENT], preferred_element_type=jnp.float32)
    return finish(o_lat.astype(jnp.bfloat16), hidden, w_uv, w_o)


def slot_positions(owners, pool_size, slot_count):
    dev_ids = jnp.arange(pool_size, dtype=jnp.int32)
    owner_hits = (owners[:, None] == dev_ids[None, :]).astype(jnp.int32)
    earlier = jnp.cumsum(owner_hits, axis=0) - owner_hits
    slot_rank = jnp.sum(earlier * owner_hits, axis=1)
    return jnp.where(owners >= 0, owners * slot_count + slot_rank, pool_size * slot_count)


def write_new_pages(new_keys, wr_table, cache_c, cache_kr, pool_size):
    cache_pages = cache_c.shape[1]
    write_count = wr_table.shape[0] * wr_table.shape[1]
    write_slots = -(-write_count // pool_size)
    write_pos = slot_positions(wr_table[:, :, 0].reshape(write_count), pool_size, write_slots)
    new_pages = new_keys.reshape(write_count, PAGE_LEN, LATENT + ROPE_DIM)
    out_pages = jnp.zeros((pool_size * write_slots, PAGE_LEN, LATENT + ROPE_DIM), jnp.bfloat16).at[write_pos].set(new_pages)
    out_ids = jnp.full((pool_size * write_slots,), cache_pages, jnp.int32).at[write_pos].set(wr_table[:, :, 1].reshape(write_count))
    in_pages = lax.all_to_all(out_pages, "pool", 0, 0, tiled=True)
    in_ids = lax.all_to_all(out_ids, "pool", 0, 0, tiled=True)
    cache_c_out = cache_c[0].at[in_ids].set(in_pages[..., :LATENT], mode="drop")[None]
    cache_kr_out = cache_kr[0].at[in_ids].set(in_pages[..., LATENT:], mode="drop")[None]
    return cache_c_out, cache_kr_out


def solution(mesh):
    pool_size = mesh.shape["pool"]

    def device_step(hidden, pre_len, pre_table, wr_table, cache_c, cache_kr, w_q, w_dkv, g_kv, w_uk, w_uv, w_o):
        req_count = hidden.shape[0]
        table_pages = pre_table.shape[1]
        entries = req_count * table_pages
        read_slots = max(1, (2 * entries) // pool_size)
        q_cat, new_keys = chunk_project(hidden, pre_len, w_q, w_dkv, g_kv, w_uk)
        read_pos = slot_positions(pre_table[:, :, 0].reshape(entries), pool_size, read_slots)
        asked_ids = jnp.zeros((pool_size * read_slots,), jnp.int32).at[read_pos].set(pre_table[:, :, 1].reshape(entries), mode="drop")
        served_ids = lax.all_to_all(asked_ids, "pool", 0, 0, tiled=True)
        served = jnp.concatenate([cache_c[0][served_ids], cache_kr[0][served_ids]], axis=-1)
        fetched = lax.all_to_all(served, "pool", 0, 0, tiled=True)
        prefix_keys = fetched[jnp.minimum(read_pos, pool_size * read_slots - 1)]
        prefix_keys = prefix_keys.reshape(req_count, table_pages * PAGE_LEN, LATENT + ROPE_DIM)
        cache_c_out, cache_kr_out = write_new_pages(new_keys, wr_table, cache_c, cache_kr, pool_size)
        hidden_out = attend(q_cat, new_keys, prefix_keys, pre_len, hidden, w_uv, w_o)
        return hidden_out, cache_c_out, cache_kr_out

    row_spec = P("pool")
    rep_spec = P()
    return jax.shard_map(device_step, mesh=mesh, in_specs=(row_spec,) * 6 + (rep_spec,) * 6, out_specs=(row_spec, row_spec, row_spec), check_vma=False)
```

profile of v0, /device:TPU:0, one launch (start us, length us, event | category | flops | bytes accessed | tf_op | source)
XLA Modules:
  0.0 663.2 jit_solution(10632219175221309555)
XLA Ops:
  0.6 1.0 copy.75
  1.7 1.0 copy.74
  2.7 0.8 fusion.60
  3.4 0.6 reduce-window.6
  4.0 0.2 slice_reduce_fusion
  4.3 0.1 fusion.51
  4.4 0.7 compare_select_fusion.1
  5.1 1.4 scatter_custom_fusion
  6.5 0.7 all_to_all.24
  7.1 4.3 all-to-all-start
  11.4 1.3 fusion.61
  14.7 0.7 convert_element_type.102
  15.4 1.8 convolution_bitcast_fusion
  17.2 0.1 multiply_reduce_fusion
  17.3 1.4 and_reduce_fusion
  18.7 0.2 fusion.47
  18.9 0.1 multiply_convert_fusion
  19.1 0.9 broadcast_in_dim.31
  20.0 1.3 fusion.38
  21.9 0.6 all_to_all.28
  22.5 0.5 constant_dynamic-update-slice_fusion
  23.0 2.9 all-to-all-start.2
  26.0 0.5 broadcast.392
  26.5 0.7 reduce.21
  27.2 13.2 %gather_fusion.1 = bf16[512,64,64]{2,1,0:T(8,128)(2,1)} fusion(bf16[5,64,64]{2,1,0:T(8,128)(2,1)S(1)} %bitcast.149, s32[1024]{0:T(1024)S(1)} %pad_clamp_fusion.1), kind=kCustom, calls=%fused_computation.1 | custom fusion | bytes 8390656 | tf_op jit(solution)/shard_map/gather | solution.py:107
  40.4 15.3 %gather_fusion = bf16[512,64,512]{2,1,0:T(8,128)(2,1)} fusion(bf16[5,64,512]{2,1,0:T(8,128)(2,1)S(1)} %bitcast.146, s32[1024]{0:T(1024)S(1)} %pad_clamp_fusion.1), kind=kCustom, calls=%fused_computation | custom fusion | bytes 67110912 | tf_op jit(solution)/shard_map/gather | solution.py:107
  55.8 3.2 all-to-all-start.3
  58.9 28.4 %pad_maximum_fusion = bf16[512,64,576]{2,1,0:T(8,128)(2,1)} fusion(bf16[512,64,64]{2,1,0:T(8,128)(2,1)} %gather_fusion.1, bf16[512,64,512]{2,1,0:T(8,128)(2,1)} %gather_fusion), kind=kLoop, calls=%fused_computation.12 | loop fusion | flops 75497472 | bytes 75497472 | tf_op jit(solution)/shard_map/concatenate | solution.py:107
  87.4 6.9 %all-to-all-start.1 = ((bf16[512,64,576]{2,1,0:T(8,128)(2,1)}), bf16[512,64,576]{2,1,0:T(8,128)(2,1)}, u32[]{:S(2)}, u32[]{:S(2)}) async-start(bf16[512,64,576]{2,1,0:T(8,128)(2,1)} %pad_maximum_fusion), calls=%async_computation.1 | async-start | bytes 83886080 | tf_op jit(solution)/shard_map/all_to_all | solution.py:108
  94.3 6.9 %convolution_convert_fusion = bf16[64,3072]{1,0:T(8,128)(2,1)S(1)} fusion(bf16[2048,3072]{1,0:T(8,128)(2,1)} %param.22, bf16[1,64,2048]{2,1,0:T(8,128)(2,1)S(1)} %copy-done.4), kind=kOutput, calls=%fused_computation.17 | convolution fusion | flops 805502976 | bytes 13238272 | tf_op jit(solution)/shard_map/dot_general | solution.py:32
  101.2 0.6 reshape.579
  102.0 0.2 multiply_cosine_fusion.1
  102.2 2.6 fusion.14
  104.9 0.3 subtract_convert_fusion
  105.2 0.7 copy-done.6
  105.9 0.9 fusion.62
  106.7 0.2 reduce.16
  107.0 0.8 scatter_fusion.1
  107.9 0.8 scatter_fusion
  108.7 439.5 %all-to-all-done.1 = bf16[512,64,576]{2,1,0:T(8,128)(2,1)} async-done(((bf16[512,64,576]{2,1,0:T(8,128)(2,1)}), bf16[512,64,576]{2,1,0:T(8,128)(2,1)}, u32[]{:S(2)}, u32[]{:S(2)}) %all-to-all-start.1) | async-done | bytes 37748768 | tf_op jit(solution)/shard_map/all_to_all | solution.py:108
  548.2 14.8 %gather_fusion.2 = bf16[256,64,576]{2,1,0:T(8,128)(2,1)} fusion(bf16[512,64,576]{2,1,0:T(8,128)(2,1)} %all-to-all-done.1, s32[1024]{0:T(1024)S(1)} %pad_clamp_fusion), kind=kCustom, calls=%fused_computation.2 | custom fusion | bytes 37749760 | tf_op jit(solution)/shard_map/gather | solution.py:109
  563.0 37.2 %bitcast_reduce_fusion = (f32[16,64]{1,0:T(8,128)S(1)}, f32[16384,64,16]{0,1,2:T(8,128)}) fusion(pred[16384]{0:T(1024)(128)(4,1)S(1)} %iota_compare_fusion, bf16[16384,576,1]{1,0,2:T(8,128)(2,1)} %bitcast.152, bf16[1,64,16,32]{3,1,2,0:T(8,128)(2,1)S(1)} %get-tuple-element.30, bf16[1,64,16,32]{3,1,2,0:T(8,128)(2,1)S(1)} %get-tuple-element.29, ...), kind=kOutput, calls=%fused_computation.7 | convolution fusion | flops 19381223424 | bytes 87183360 | tf_op jit(solution)/shard_map/rchk,rjk->rhcj/dot_general | solution.py:57
  600.1 0.1 fusion.25
  600.3 21.7 %fusion.1 = f32[16,64]{1,0:T(8,128)S(1)} fusion(f32[16384,64,16]{0,1,2:T(8,128)} %get-tuple-element.40, f32[16,64]{1,0:T(8,128)S(1)} %max.8, pred[16384]{0:T(1024)(128)(4,1)S(1)} %iota_compare_fusion), kind=kLoop, calls=%fused_computation.11 | loop fusion | flops 67107840 | bytes 67133440 | tf_op jit(solution)/shard_map/reduce_sum | solution.py:66
  622.0 31.9 %fusion.2 = f32[16,64,512]{2,1,0:T(8,128)} fusion(f32[16384,64,16]{0,1,2:T(8,128)} %get-tuple-element.40, f32[16,64]{1,0:T(8,128)S(1)} %add.123, f32[16,64]{1,0:T(8,128)S(1)} %max.8, pred[16384]{0:T(1024)(128)(4,1)S(1)} %iota_compare_fusion, bf16[1,16384,576]{2,1,0:T(8,128)(2,1)} %bitcast.153), kind=kOutput, calls=%fused_computation.13 | convolution fusion | flops 17263755264 | bytes 86007808 | tf_op jit(solution)/shard_map/rhcj,rjl->rhcl/dot_general | solution.py:67
  653.9 3.4 fusion.22
  657.3 0.2 copy.41
  657.5 5.7 fusion.6
  (44 shorter events, 0.6 us)
Async XLA Ops:
  0.6 14.8 %copy-start = (bf16[2048,576]{0,1:T(8,128)(2,1)S(1)}, bf16[2048,576]{0,1:T(8,128)(2,1)}, u32[]{:S(2)}) copy-start(bf16[2048,576]{0,1:T(8,128)(2,1)} %param.23) | copy-start | bytes 7077892
  7.1 15.9 %all-to-all-start = ((s32[8,64,1]{1,2,0:T(1,128)}), s32[8,64,1]{1,2,0:T(1,128)S(1)}, u32[]{:S(2)}, u32[]{:S(2)}) async-start(s32[8,64,1]{1,2,0:T(1,128)} %bitcast.12), calls=%async_computation | async-start | bytes 8192 | tf_op jit(solution)/shard_map/all_to_all | solution.py:106
  19.0 86.2 %copy-start.8 = (bf16[1,64,512]{2,1,0:T(8,128)(2,1)}, bf16[1,64,512]{2,1,0:T(8,128)(2,1)S(1)}, u32[]{:S(2)}) copy-start(bf16[1,64,512]{2,1,0:T(8,128)(2,1)S(1)} %multiply_convert_fusion) | copy-start | bytes 196612
  23.0 32.8 %all-to-all-start.2 = ((s32[8,1,1]{2,1,0:T(1,128)}), s32[8,1,1]{2,1,0:T(1,128)S(1)}, u32[]{:S(2)}, u32[]{:S(2)}) async-start(s32[8,1,1]{2,1,0:T(1,128)} %constant_dynamic-update-slice_fusion), calls=%async_computation.2 | async-start | bytes 8192 | tf_op jit(solution)/shard_map/all_to_all | solution.py:89
  55.8 31.6 %all-to-all-start.3 = ((bf16[8,64,576]{2,1,0:T(8,128)(2,1)}), bf16[8,64,576]{2,1,0:T(8,128)(2,1)S(1)}, u32[]{:S(2)}, u32[]{:S(2)}) async-start(bf16[8,64,576]{2,1,0:T(8,128)(2,1)} %fusion.38), calls=%async_computation.3 | async-start | bytes 1310720 | tf_op jit(solution)/shard_map/all_to_all | solution.py:88
  87.4 7.0 %copy-start.4 = (bf16[1,64,2048]{2,1,0:T(8,128)(2,1)S(1)}, bf16[1,64,2048]{2,1,0:T(8,128)(2,1)}, u32[]{:S(2)}) copy-start(bf16[1,64,2048]{2,1,0:T(8,128)(2,1)} %param.16) | copy-start | bytes 786436
  87.4 460.8 %all-to-all-start.1 = ((bf16[512,64,576]{2,1,0:T(8,128)(2,1)}), bf16[512,64,576]{2,1,0:T(8,128)(2,1)}, u32[]{:S(2)}, u32[]{:S(2)}) async-start(bf16[512,64,576]{2,1,0:T(8,128)(2,1)} %pad_maximum_fusion), calls=%async_computation.1 | async-start | bytes 83886080 | tf_op jit(solution)/shard_map/all_to_all | solution.py:108
  104.8 1.0 copy-start.6
  107.8 455.2 %copy-start.3 = (bf16[5,64,64]{2,1,0:T(8,128)(2,1)}, bf16[5,64,64]{2,1,0:T(8,128)(2,1)S(1)}, u32[]{:S(2)}) copy-start(bf16[5,64,64]{2,1,0:T(8,128)(2,1)S(1)} %scatter_fusion.1) | copy-start | bytes 122884
  108.6 454.3 %copy-start.2 = (bf16[5,64,512]{2,1,0:T(8,128)(2,1)}, bf16[5,64,512]{2,1,0:T(8,128)(2,1)S(1)}, u32[]{:S(2)}) copy-start(bf16[5,64,512]{2,1,0:T(8,128)(2,1)S(1)} %scatter_fusion) | copy-start | bytes 983044
  108.7 454.3 %copy-start.7 = (bf16[1,64,16,512]{3,1,2,0:T(8,128)(2,1)S(1)}, bf16[1,64,16,512]{3,1,2,0:T(8,128)(2,1)}, u32[]{:S(2)}) copy-start(bf16[1,64,16,512]{3,1,2,0:T(8,128)(2,1)} %copy-done.6) | copy-start | bytes 3145732
  622.0 31.9 %copy-start.9 = (bf16[1,64,512]{2,1,0:T(8,128)(2,1)S(1)}, bf16[1,64,512]{2,1,0:T(8,128)(2,1)}, u32[]{:S(2)}) copy-start(bf16[1,64,512]{2,1,0:T(8,128)(2,1)} %copy-done.8) | copy-start | bytes 196612
  622.0 35.5 %copy-start.5 = (bf16[1,64,2048]{2,1,0:T(8,128)(2,1)S(1)}, bf16[1,64,2048]{2,1,0:T(8,128)(2,1)}, u32[]{:S(2)}) copy-start(bf16[1,64,2048]{2,1,0:T(8,128)(2,1)} %param.16) | copy-start | bytes 786436
  622.0 41.2 %copy-start.1 = (bf16[2048,576]{0,1:T(8,128)(2,1)S(1)}, bf16[2048,576]{0,1:T(8,128)(2,1)}, u32[]{:S(2)}) copy-start(bf16[2048,576]{0,1:T(8,128)(2,1)} %param.23) | copy-start | bytes 7077892
where the time goes:
time: 664 us; the launch traced here: 663 us
  waiting for transfers between devices  439 us (66%)
  matrix products  90.3 us (14%)
  other arithmetic  57 us (9%)
  local copies, waits for them, and re-layouts  55.5 us (8%)
  starting transfers between devices  17.3 us (3%)
    all_to_all x1, waiting for transfers between devices, device_step(): fetched = lax.all_to_all(served, 'pool', 0, 0, tiled=True)  439 us
    dot_general x1, matrix products, attend(): jnp.einsum('rchk,rjk->rhcj', q_cat, prefix_keys, preferred_element_type=j...  37.2 us
    dot_general x1, matrix products, attend(): jnp.einsum('rhcj,rjl->rhcl', (e_pre / denom_sum).astype(jnp.bfloat16), pr...  31.9 us
    concatenate x1, other arithmetic, device_step(): jnp.concatenate([cache_c[0][served_ids], cache_kr[0][served_ids]], axis=-1)  28.4 us
    reduce_sum x1, other arithmetic, attend(): jnp.sum(e_pre, axis=-1, keepdims=True)  21.7 us
    gather x1, local copies, waits for them, and re-layouts, device_step(): cache_c[0][served_ids]  15.3 us
    gather x1, local copies, waits for them, and re-layouts, device_step(): prefix_keys = fetched[jnp.minimum(read_pos, pool_size * read_slots - 1)]  14.8 us
  transfers between devices with their start and end apart: 4, of which 1 were waited for; matrix products, arithmetic and copies ran while one was open for 12% of the time, Pallas kernels for 0%

commit v1 on v0

v1 whole, which is shorter than its diff:
```python
import functools
import math

import jax
import jax.numpy as jnp
import numpy as np
from jax import lax
from jax.experimental import pallas as pl
from jax.experimental.pallas import tpu as pltpu
from jax.sharding import PartitionSpec as P

BF = jnp.bfloat16
F32 = jnp.float32
MESH = pl.DeviceIdType.MESH

TOK = 64
DM = 2048
NH = 16
LAT = 512
RD = 64
ND = 128
HQ = ND + RD
ROWS = NH * TOK
EPS = 1e-6
GROUP = 4
GCOLS = GROUP * HQ
NGROUP = NH // GROUP
BLK = 256
SCALE2 = float((ND + RD) ** -0.5 * math.log2(math.e))
INV_FREQ = [float(np.float32(10000.0 ** (-k / 32.0))) for k in range(32)]

CHUNKS = (
    ((0, 0), (0, 1)),
    ((1, 0), (1, 1)),
    ((2, 0), (4, 1)),
    ((3, 0), (5, 1)),
    ((2, 1), (4, 0)),
    ((3, 1), (5, 0)),
    ((6, 0), (6, 1)),
    ((7, 0), (7, 1)),
)

FLOWS = {
    "x0": (0, 0, 2, 0, "x"),
    "x1": (0, 1, 4, 0, "x"),
    "y1": (0, 1, 2, 1, "y"),
    "y0": (0, 0, 4, 1, "y"),
    "p0": (0, 0, 1, 0, "p"),
    "p1": (0, 1, 1, 1, "p"),
    "dy": (2, 0, 6, 0, "y"),
    "dx": (2, 1, 6, 1, "x"),
    "p20": (2, 0, 3, 0, "p"),
    "p21": (2, 1, 3, 1, "p"),
    "p40": (4, 0, 5, 0, "p"),
    "p41": (4, 1, 5, 1, "p"),
    "p60": (6, 0, 7, 0, "p"),
    "p61": (6, 1, 7, 1, "p"),
}
FLOW_ID = {name: i for i, name in enumerate(FLOWS)}
NF = 2 * len(FLOWS)

NEWS = {
    "nx": (0, 2, "x", (0, 1), True),
    "ny": (0, 4, "y", (0, 1), True),
    "np": (0, 1, "p", (0, 1), True),
    "n2p": (2, 3, "p", (0, 1), True),
    "n4p": (4, 5, "p", (0, 1), True),
    "ndy": (2, 6, "y", (0,), False),
    "ndx": (4, 6, "x", (1,), True),
    "n6p": (6, 7, "p", (0, 1), True),
}
NEW_ID = {}
for _name, (_s, _t, _d, _h, _k) in NEWS.items():
    for _part in ("c", "k"):
        if _part == "c" or _k:
            NEW_ID[(_name, _part)] = NF + len(NEW_ID)
NSEM = NF + len(NEW_ID)


def body(x_hbm, plen_hbm, tbl_hbm, wt_hbm, cc_hbm, ckr_hbm, wq_hbm, wdkv_hbm, g_hbm, wuk_hbm, wuv_hbm, wo_hbm,
         y_hbm, cco_hbm, ckro_hbm,
         x_v, plen_s, tbl_v, wt_s, ckr_v, wq_v, wdkv_v, g_v, wuk_v, wuv_v, wo_v,
         kc, krp, nc, nk, wukt, wuvt, q_s, qr_s, o_s, m_s, l_s, bias_s, ob_s, y_v, pc_v, pk_v,
         loc_sem, send_sem, recv_sem):
    me = lax.axis_index("pool")
    core = lax.rem(me, 2)
    cx = lax.rem(lax.div(me, 2), 2)
    cy = lax.div(me, 4)
    fp = 1 - 2 * core
    fx = 2 - 4 * cx
    fy = 4 - 8 * cy
    peer = {"p": me + fp, "x": me + fx, "y": me + fy}

    n_loc = [0]

    def local(src, dst):
        cp = pltpu.make_async_copy(src, dst, loc_sem.at[n_loc[0]])
        n_loc[0] += 1
        cp.start()
        return cp

    ld_kr = local(ckr_hbm, ckr_v)
    ld_c = [local(cc_hbm.at[p], kc.at[0, p % 2, p // 2]) for p in range(4)]
    ld_x = local(x_hbm, x_v)
    ld_dkv = local(wdkv_hbm, wdkv_v)
    ld_small = [local(plen_hbm, plen_s), local(tbl_hbm, tbl_v), local(wt_hbm, wt_s), local(g_hbm, g_v)]
    ld_uk = local(wuk_hbm, wuk_v)
    ld_q = [local(wq_hbm.at[:, pl.ds(g * GCOLS, GCOLS)], wq_v.at[g]) for g in range(NGROUP)]
    ld_uv = local(wuv_hbm, wuv_v)
    ld_o = local(wo_hbm, wo_v)

    barrier = pltpu.get_barrier_semaphore()
    for d in ("p", "x", "y"):
        pl.semaphore_signal(barrier, inc=1, device_id=(peer[d],), device_id_type=MESH)

    lane = lax.broadcasted_iota(jnp.int32, (TOK, 128), 1)
    low = lane < RD

    ld_kr.wait()
    for h in range(2):
        krp[0, h] = jnp.concatenate([ckr_v[2 * h], ckr_v[2 * h + 1]], axis=-1)

    def page_copies(name):
        sc, sh, tc, th, d = FLOWS[name]
        i = 2 * FLOW_ID[name]
        return [
            pltpu.make_async_remote_copy(src_ref=kc.at[sc, :, sh], dst_ref=kc.at[tc, :, th], send_sem=send_sem.at[i],
                                         recv_sem=recv_sem.at[i], device_id=(peer[d],), device_id_type=MESH),
            pltpu.make_async_remote_copy(src_ref=krp.at[sc, sh], dst_ref=krp.at[tc, th], send_sem=send_sem.at[i + 1],
                                         recv_sem=recv_sem.at[i + 1], device_id=(peer[d],), device_id_type=MESH),
        ]

    def new_copies(name):
        s, t, d, halves, tag = NEWS[name]
        rows = slice(halves[0], halves[-1] + 1)
        i = NEW_ID[(name, "c")]
        out = [pltpu.make_async_remote_copy(src_ref=nc.at[s, rows], dst_ref=nc.at[t, rows], send_sem=send_sem.at[i],
                                            recv_sem=recv_sem.at[i], device_id=(peer[d],), device_id_type=MESH)]
        if tag:
            i = NEW_ID[(name, "k")]
            out.append(pltpu.make_async_remote_copy(src_ref=nk.at[s], dst_ref=nk.at[t], send_sem=send_sem.at[i],
                                                    recv_sem=recv_sem.at[i], device_id=(peer[d],), device_id_type=MESH))
        return out

    started = []

    def send(name):
        for cp in (page_copies if name in FLOWS else new_copies)(name):
            cp.start()
            started.append(cp)

    def arrived(name):
        for cp in (page_copies if name in FLOWS else new_copies)(name):
            cp.wait_recv()

    pl.semaphore_wait(barrier, 3)
    for cp in ld_c:
        cp.wait()
    for name in ("x0", "y1", "p0", "p1", "x1", "y0"):
        send(name)

    out_cps = [local(kc.at[0, p % 2, p // 2], cco_hbm.at[p]) for p in range(4)]
    out_cps.append(local(ckr_v.at[pl.ds(0, 4)], ckro_hbm.at[pl.ds(0, 4)]))

    for cp in ld_small:
        cp.wait()
    k_lane = lax.rem(lane, 32)
    freq = jnp.zeros((TOK, 128), F32)
    for k, f in enumerate(INV_FREQ):
        freq = jnp.where(k_lane == k, f, freq)
    pos = (lax.broadcasted_iota(jnp.int32, (TOK, 128), 0) + plen_s[0]).astype(F32)
    ang = pos * freq
    cos_t = jnp.cos(ang)
    sin_t = jnp.sin(ang)
    sin_t = jnp.where(lax.rem(lane, 64) < 32, -sin_t, sin_t)

    def rope2(v64):
        v = jnp.concatenate([v64, v64], axis=-1)
        return v * cos_t + pltpu.roll(v, 32, 1) * sin_t

    ld_x.wait()
    ld_dkv.wait()
    kv = lax.dot_general(x_v[...], wdkv_v[...], (((1,), (1,)), ((), ())), preferred_element_type=F32)
    latp = kv[:, :LAT]
    inv_rms = lax.rsqrt(jnp.mean(latp * latp, axis=-1, keepdims=True) + EPS)
    c_new = (latp * inv_rms * g_v[...].astype(F32)).astype(BF)
    kr_dup = rope2(kv[:, LAT:]).astype(BF)
    nc[0, 0] = c_new[:32]
    nc[0, 1] = c_new[32:]
    nk[0, pl.ds(0, 32)] = jnp.where(low[:32], kr_dup[:32], kr_dup[32:])
    nk[0, pl.ds(32, 16)] = jnp.full((16, 128), wt_s[0, 0], jnp.int32).astype(F32).astype(BF)

    tbl = tbl_v[...]
    ids = (tbl[0:1] * 4 + tbl[1:2]).astype(F32)
    ids_col = jnp.transpose(jnp.broadcast_to(ids, (128, 256)))
    seg = lax.div(lax.broadcasted_iota(jnp.int32, (1, 256), 1), 64)
    flips = {0: 0, 1: fp, 2: fx, 4: fy, 3: fp + fx, 5: fp + fy, 6: fx + fy, 7: fp + fx + fy}
    for c, ((ra, ha), (rb, hb)) in enumerate(CHUNKS):
        pa = (me + flips[ra]) * 4 + 2 * ha
        pb = (me + flips[rb]) * 4 + 2 * hb
        want = jnp.where(seg == 0, pa, jnp.where(seg == 1, pb, jnp.where(seg == 2, pa + 1, pb + 1))).astype(F32)
        parts = []
        for t in range(2):
            hit = jnp.where(ids_col == want[:, t * 128:(t + 1) * 128], 1.0, 0.0)
            parts.append(jnp.sum(hit, axis=0, keepdims=True))
        cnt = jnp.concatenate(parts, axis=-1)
        bias_s[c] = jnp.where(cnt > 0.0, jnp.log2(jnp.maximum(cnt, 1.0)), -jnp.inf)

    r_i = lax.broadcasted_iota(jnp.int32, (256, 256), 0)
    c_i = lax.broadcasted_iota(jnp.int32, (256, 256), 1)
    perm = (r_i == lax.rem(c_i, 16) * 16 + lax.div(c_i, 16)).astype(F32).astype(BF)

    def reorder(src, dst):
        def step(b, carry):
            for u in range(4):
                blk = b * 4 + u
                rows = src[pl.ds(pl.multiple_of(blk * 256, 256), 256), :]
                t = jnp.dot(perm, rows, preferred_element_type=F32).astype(BF)
                dst[:, pl.ds(pl.multiple_of(blk * 16, 16), 16), :] = t.reshape(NH, 16, 128)
            return carry
        lax.fori_loop(0, 8, step, 0)

    ld_uk.wait()
    reorder(wuk_v, wukt)

    for g in range(NGROUP):
        ld_q[g].wait()
        qg = jnp.dot(x_v[...], wq_v[g], preferred_element_type=F32).astype(BF).astype(F32)
        for k in range(GROUP):
            h = g * GROUP + k
            nope = qg[:, k * HQ:k * HQ + ND].astype(BF)
            qr_s[pl.ds(h * TOK, TOK), :] = rope2(qg[:, k * HQ + ND:(k + 1) * HQ]).astype(BF)
            q_s[pl.ds(h * TOK, TOK), :] = lax.dot_general(
                nope, wukt[h], (((1,), (1,)), ((), ())), preferred_element_type=F32).astype(BF)

    NT = (((1,), (1,)), ((), ()))
    kr_low = jnp.where(low, kr_dup.astype(F32), 0.0).astype(BF)
    row_tok = lax.rem(lax.broadcasted_iota(jnp.int32, (BLK, TOK), 0), TOK)
    key_tok = lax.broadcasted_iota(jnp.int32, (BLK, TOK), 1)
    causal = key_tok <= row_tok
    for b in range(ROWS // BLK):
        rows = pl.ds(b * BLK, BLK)
        s = lax.dot_general(q_s[rows, :], c_new, NT, preferred_element_type=F32)
        s = s + lax.dot_general(qr_s[rows, :], kr_low, NT, preferred_element_type=F32)
        t = jnp.where(causal, s * SCALE2, -jnp.inf)
        mx = jnp.max(t, axis=-1, keepdims=True)
        p = jnp.exp2(t - mx)
        m_s[rows, :] = jnp.broadcast_to(mx, (BLK, 128))
        l_s[rows, :] = jnp.concatenate([p, jnp.zeros_like(p)], axis=-1)
        o_s[rows, :] = jnp.dot(p.astype(BF), c_new, preferred_element_type=F32)

    lane2 = lax.broadcasted_iota(jnp.int32, (128, 128), 1)

    def attend(c):
        keys = kc[c].reshape(256, LAT)
        kp = krp[c].reshape(128, 128).astype(F32)
        kbd = jnp.concatenate([jnp.where(lane2 < RD, kp, 0.0), jnp.where(lane2 < RD, 0.0, kp)], axis=0).astype(BF)
        bias = bias_s[c]
        for b in range(ROWS // BLK):
            rows = pl.ds(b * BLK, BLK)
            s = lax.dot_general(q_s[rows, :], keys, NT, preferred_element_type=F32)
            s = s + lax.dot_general(qr_s[rows, :], kbd, NT, preferred_element_type=F32)
            t = s * SCALE2 + bias
            mx = jnp.max(jnp.maximum(t[:, :128], t[:, 128:]), axis=-1, keepdims=True)
            m_old = m_s[rows, :]
            m_new = jnp.maximum(m_old, jnp.broadcast_to(mx, (BLK, 128)))
            alpha = jnp.exp2(m_old - m_new)
            p = jnp.exp2(t - jnp.concatenate([m_new, m_new], axis=-1))
            m_s[rows, :] = m_new
            l_s[rows, :] = l_s[rows, :] * alpha + (p[:, :128] + p[:, 128:])
            a4 = jnp.concatenate([alpha] * 4, axis=-1)
            o_s[rows, :] = o_s[rows, :] * a4 + jnp.dot(p.astype(BF), keys, preferred_element_type=F32)

    for name in ("x0", "y1"):
        arrived(name)
    for name in ("dy", "dx", "p20", "p21"):
        send(name)
    for name in ("nx", "ny", "np"):
        send(name)
    attend(0)
    for name in ("p0", "p1"):
        arrived(name)
    attend(1)
    attend(2)
    ld_uv.wait()
    reorder(wuv_v, wuvt)
    for name in ("x1", "y0"):
        arrived(name)
    for name in ("p40", "p41"):
        send(name)
    attend(4)
    for name in ("p20", "p21"):
        arrived(name)
    attend(3)
    for name in ("p40", "p41"):
        arrived(name)
    attend(5)
    for name in ("dy", "dx"):
        arrived(name)
    for name in ("p60", "p61"):
        send(name)
    for name in ("nx", "ny"):
        arrived(name)
    for name in ("ndy", "ndx", "n2p", "n4p"):
        send(name)
    attend(6)
    for name in ("p60", "p61"):
        arrived(name)
    attend(7)

    for h in range(NH):
        rows = pl.ds(h * TOK, TOK)
        denom = jnp.sum(l_s[rows, :], axis=-1, keepdims=True)
        ol = (o_s[rows, :] / denom).astype(BF)
        ob_s[:, pl.ds(h * ND, ND)] = jnp.dot(ol, wuvt[h], preferred_element_type=F32).astype(BF)
    for name in ("ndy", "ndx"):
        arrived(name)
    send("n6p")
    ld_o.wait()
    NB = 512

    def out_step(j, carry):
        cols = pl.ds(pl.multiple_of(j * NB, NB), NB)
        acc = jnp.dot(ob_s[...], wo_v[:, cols], preferred_element_type=F32)
        y_v[:, cols] = (x_v[:, cols].astype(F32) + acc).astype(BF)
        return carry
    lax.fori_loop(0, DM // NB, out_step, 0)
    y_cp = local(y_v, y_hbm)

    for name in ("np", "n2p", "n4p", "n6p"):
        arrived(name)
    mine = me.astype(F32)
    pc = [jnp.zeros((32, LAT), F32) for _ in range(2)]
    pk = jnp.zeros((32, 128), F32)
    for r in range(8):
        hit = nk[r, pl.ds(32, 16)].astype(F32)
        hit = jnp.concatenate([hit, hit], axis=0) == mine
        pk = jnp.where(hit, nk[r, pl.ds(0, 32)].astype(F32), pk)
        hit4 = jnp.concatenate([hit] * 4, axis=-1)
        for u in range(2):
            pc[u] = jnp.where(hit4, nc[r, u].astype(F32), pc[u])
    pc_v[pl.ds(0, 32), :] = pc[0].astype(BF)
    pc_v[pl.ds(32, 32), :] = pc[1].astype(BF)
    pkb = pk.astype(BF)
    pk_v[pl.ds(0, 32), :] = pkb[:, :RD]
    pk_v[pl.ds(32, 32), :] = pkb[:, RD:]
    out_cps.append(local(pc_v, cco_hbm.at[4]))
    out_cps.append(local(pk_v, ckro_hbm.at[4]))
    for cp in started:
        cp.wait_send()
    y_cp.wait()
    for cp in out_cps:
        cp.wait()


def fused(x, plen, tbl, wt, cc, ckr, wq, wdkv, g, wuk, wuv, wo):
    any_spec = pl.BlockSpec(memory_space=pl.ANY)
    dma = pltpu.SemaphoreType.DMA
    return pl.pallas_call(
        body,
        name="mla_prefill",
        out_shape=(
            jax.ShapeDtypeStruct((TOK, DM), BF),
            jax.ShapeDtypeStruct((5, TOK, LAT), BF),
            jax.ShapeDtypeStruct((5, TOK, RD), BF),
        ),
        in_specs=[any_spec] * 12,
        out_specs=(any_spec,) * 3,
        scratch_shapes=[
            pltpu.VMEM((TOK, DM), BF),
            pltpu.SMEM((1,), jnp.int32),
            pltpu.VMEM((2, 256), jnp.int32),
            pltpu.SMEM((1, 2), jnp.int32),
            pltpu.VMEM((5, TOK, RD), BF),
            pltpu.VMEM((NGROUP, DM, GCOLS), BF),
            pltpu.VMEM((LAT + RD, DM), BF),
            pltpu.VMEM((1, LAT), BF),
            pltpu.VMEM((LAT * NH, ND), BF),
            pltpu.VMEM((LAT * NH, ND), BF),
            pltpu.VMEM((DM, DM), BF),
            pltpu.VMEM((8, 2, 2, TOK, LAT), BF),
            pltpu.VMEM((8, 2, TOK, 128), BF),
            pltpu.VMEM((8, 2, 32, LAT), BF),
            pltpu.VMEM((8, 48, 128), BF),
            pltpu.VMEM((NH, LAT, ND), BF),
            pltpu.VMEM((NH, LAT, ND), BF),
            pltpu.VMEM((ROWS, LAT), BF),
            pltpu.VMEM((ROWS, 128), BF),
            pltpu.VMEM((ROWS, LAT), F32),
            pltpu.VMEM((ROWS, 128), F32),
            pltpu.VMEM((ROWS, 128), F32),
            pltpu.VMEM((8, 1, 256), F32),
            pltpu.VMEM((TOK, DM), BF),
            pltpu.VMEM((TOK, DM), BF),
            pltpu.VMEM((TOK, LAT), BF),
            pltpu.VMEM((TOK, RD), BF),
            dma((32,)),
            dma((NSEM,)),
            dma((NSEM,)),
        ],
        compiler_params=pltpu.CompilerParams(collective_id=0, has_side_effects=True, vmem_limit_bytes=60 * 1024 * 1024),
    )(x, plen, tbl, wt, cc, ckr, wq, wdkv, g, wuk, wuv, wo)


def solution(mesh):
    def device_step(hidden, pre_len, pre_table, wr_table, cache_c, cache_kr, w_q, w_dkv, g_kv, w_uk, w_uv, w_o):
        y, c_out, kr_out = fused(
            hidden.reshape(TOK, DM), pre_len, pre_table.reshape(256, 2).T, wr_table.reshape(1, 2), cache_c[0], cache_kr[0],
            w_q, w_dkv.T, g_kv.reshape(1, LAT), w_uk.reshape(LAT * NH, ND), w_uv.reshape(LAT * NH, ND), w_o)
        return y[None], c_out[None], kr_out[None]

    row = P("pool")
    rep = P()
    return jax.shard_map(device_step, mesh=mesh, in_specs=(row,) * 6 + (rep,) * 6, out_specs=(row, row, row), check_vma=False)
```

time: 664 us -> 43.2 us (0.07)
  waiting for transfers between devices: 439 us -> 0 us
  matrix products: 90.3 us -> 0 us
  other arithmetic: 57 us -> 0 us
  local copies, waits for them, and re-layouts: 55.5 us -> 6.18 us
  Pallas kernels: 0 us -> 35.5 us
  starting transfers between devices: 17.3 us -> 0 us
    all_to_all x4 -> x0, waiting for transfers between devices: 439 us -> none  [the longest x1 439 us: device_step(): fetched = lax.all_to_all(served, 'pool', 0, 0, tiled=True)]
    dot_general x8 -> x0, matrix products: 90.3 us -> none  [the longest x1 37.2 us: attend(): jnp.einsum('rchk,rjk->rhcj', q_cat, prefix_keys, preferred_element_type=j...]
    gather x3 -> x0, local copies, waits for them, and re-layouts: 43.4 us -> none  [the longest x1 15.3 us: device_step(): cache_c[0][served_ids]]
    pallas_call x0 -> x1, Pallas kernels: none -> 35.5 us  [fused(): pl.pallas_call(body, name='mla_prefill', out_shape=(jax.ShapeDtypeStruct(...]
    concatenate x2 -> x0, other arithmetic: 28.5 us -> none  [the longest x1 28.4 us: device_step(): jnp.concatenate([cache_c[0][served_ids], cache_kr[0][served_ids]], axis=-1)]
    reduce_sum x4 -> x0, other arithmetic: 22 us -> none  [the longest x1 21.7 us: attend(): jnp.sum(e_pre, axis=-1, keepdims=True)]
    all_to_all x4 -> x0, starting transfers between devices: 17.3 us -> none  [the longest x1 6.94 us: device_step(): fetched = lax.all_to_all(served, 'pool', 0, 0, tiled=True)]
  transfers between devices with their start and end apart: 4 -> 0, of which waited for: 1 -> 0; matrix products, arithmetic and copies ran while one was open for 12% -> 0% of each run, Pallas kernels for 0% -> 0%
where the time goes in v1:
time: 43.2 us; the launch traced here: 42.9 us
  Pallas kernels  35.5 us (82%)
  local copies, waits for them, and re-layouts  6.18 us (14%)
  between operations  1.29 us (3%)
    pallas_call x1, Pallas kernels, fused(): pl.pallas_call(body, name='mla_prefill', out_shape=(jax.ShapeDtypeStruct(...  35.5 us
    unnamed x3, local copies, waits for them, and re-layouts  4.92 us
    reshape x1, local copies, waits for them, and re-layouts, device_step(): g_kv.reshape(1, LAT)  1.26 us

profile of v1, /device:TPU:0, one launch (start us, length us, event | category | flops | bytes accessed | tf_op | source)
XLA Modules:
  0.0 42.9 jit_solution(15379619533919343003)
XLA Ops:
  1.3 1.3 %reshape.27.g_hbm = bf16[1,512]{1,0:T(2,128)(2,1)} reshape(bf16[512]{0:T(512)(128)(2,1)} %param.20) | data formatting | bytes 2048 | tf_op jit(solution)/shard_map/reshape | solution.py:409
  2.5 35.5 %mla_prefill.1 = (bf16[64,2048]{1,0:T(8,128)(2,1)}, bf16[5,64,512]{2,1,0:T(8,128)(2,1)}, bf16[5,64,64]{2,1,0:T(8,128)(2,1)}) custom-call(bf16[64,2048]{1,0:T(8,128)(2,1)} %bitcast.18, s32[1]{0:T(128)S(6)} %copy.18.plen_hbm, s32[2,256]{1,0:T(2,128)} %bitcast.22, s32[1,2]{1,0:T(1,128)} %bitcast.23, bf16[5,64,512]{2,1,0:T(8,128)(2,1)} %bitcast.17, ...), custom_call_target="tpu_custom_call" | custom-call | tf_op jit(solution)/shard_map/mla_prefill/pallas_call | solution.py:359
  38.0 1.7 %copy.19 = bf16[1,64,2048]{2,1,0:T(8,128)(2,1)} copy(bf16[1,64,2048]{2,1,0:T(8,128)(2,1)} %bitcast.19) | data formatting | bytes 524288
  39.7 1.7 %copy.20 = bf16[1,5,64,512]{3,2,1,0:T(8,128)(2,1)} copy(bf16[1,5,64,512]{3,2,1,0:T(8,128)(2,1)} %bitcast.16) | data formatting | bytes 655360
  41.4 1.5 %copy.21 = bf16[1,5,64,64]{3,2,1,0:T(8,128)(2,1)} copy(bf16[1,5,64,64]{3,2,1,0:T(8,128)(2,1)} %bitcast.21) | data formatting | bytes 81920

commit v2 on v1

v2 whole, which is shorter than its diff:
```python
import contextlib
import math

import jax
import jax.numpy as jnp
import numpy as np
from jax import lax
from jax.experimental import pallas as pl
from jax.experimental.pallas import tpu as pltpu
from jax.sharding import PartitionSpec as P

BF = jnp.bfloat16
PROF = False
F32 = jnp.float32
MESH = pl.DeviceIdType.MESH

TOK = 64
DM = 2048
NH = 16
LAT = 512
RD = 64
ND = 128
HQ = ND + RD
ROWS = NH * TOK
EPS = 1e-6
GROUP = 4
GCOLS = GROUP * HQ
NGROUP = NH // GROUP
BLK = 256
SCALE2 = float((ND + RD) ** -0.5 * math.log2(math.e))
INV_FREQ = [float(np.float32(10000.0 ** (-k / 32.0))) for k in range(32)]

CHUNKS = (
    ((0, 0), (0, 1)),
    ((1, 0), (1, 1)),
    ((2, 0), (4, 1)),
    ((3, 0), (5, 1)),
    ((2, 1), (4, 0)),
    ((3, 1), (5, 0)),
    ((6, 0), (6, 1)),
    ((7, 0), (7, 1)),
)

FLOWS = {
    "x0": (0, 0, 2, 0, "x"),
    "x1": (0, 1, 4, 0, "x"),
    "y1": (0, 1, 2, 1, "y"),
    "y0": (0, 0, 4, 1, "y"),
    "p0": (0, 0, 1, 0, "p"),
    "p1": (0, 1, 1, 1, "p"),
    "dy": (2, 0, 6, 0, "y"),
    "dx": (2, 1, 6, 1, "x"),
    "p20": (2, 0, 3, 0, "p"),
    "p21": (2, 1, 3, 1, "p"),
    "p40": (4, 0, 5, 0, "p"),
    "p41": (4, 1, 5, 1, "p"),
    "p60": (6, 0, 7, 0, "p"),
    "p61": (6, 1, 7, 1, "p"),
}
FLOW_ID = {name: i for i, name in enumerate(FLOWS)}
NF = 2 * len(FLOWS)

NEWS = {
    "nx": (0, 2, "x", (0, 1), True),
    "ny": (0, 4, "y", (0, 1), True),
    "np": (0, 1, "p", (0, 1), True),
    "n2p": (2, 3, "p", (0, 1), True),
    "n4p": (4, 5, "p", (0, 1), True),
    "ndy": (2, 6, "y", (0,), False),
    "ndx": (4, 6, "x", (1,), True),
    "n6p": (6, 7, "p", (0, 1), True),
}
NEW_ID = {}
for _name, (_s, _t, _d, _h, _k) in NEWS.items():
    for _part in ("c", "k"):
        if _part == "c" or _k:
            NEW_ID[(_name, _part)] = NF + len(NEW_ID)
NSEM = NF + len(NEW_ID)


def scope(name):
    return jax.named_scope(name) if PROF else contextlib.nullcontext()


def body(x_hbm, plen_hbm, tbl_hbm, wt_hbm, cc_hbm, ckr_hbm, wq_hbm, wdkv_hbm, g_hbm, wuk_hbm, wuv_hbm, wo_hbm,
         y_hbm, cco_hbm, ckro_hbm,
         x_v, plen_s, tbl_v, wt_s, ckr_v, wq_v, wdkv_v, g_v, wuk_v, wuv_v, wo_v,
         kc, krp, nc, nk, wukt, wuvt, q_s, qr_s, s_s, o_s, m_s, l_s, bias_s, ob_s, y_v, pc_v, pk_v,
         loc_sem, send_sem, recv_sem):
    me = lax.axis_index("pool")
    core = lax.rem(me, 2)
    cx = lax.rem(lax.div(me, 2), 2)
    cy = lax.div(me, 4)
    fp = 1 - 2 * core
    fx = 2 - 4 * cx
    fy = 4 - 8 * cy
    peer = {"p": me + fp, "x": me + fx, "y": me + fy}

    barrier = pltpu.get_barrier_semaphore()
    for d in ("p", "x", "y"):
        pl.semaphore_signal(barrier, inc=1, device_id=(peer[d],), device_id_type=MESH)

    n_loc = [0]

    def local(src, dst):
        cp = pltpu.make_async_copy(src, dst, loc_sem.at[n_loc[0]])
        n_loc[0] += 1
        cp.start()
        return cp

    ld_kr = local(ckr_hbm, ckr_v)
    ld_c = [local(cc_hbm.at[p], kc.at[0, p % 2, p // 2]) for p in range(4)]
    ld_x = local(x_hbm, x_v)
    ld_dkv = local(wdkv_hbm, wdkv_v)
    ld_small = [local(plen_hbm, plen_s), local(tbl_hbm, tbl_v), local(wt_hbm, wt_s), local(g_hbm, g_v)]
    ld_uk = local(wuk_hbm, wuk_v)
    ld_q = [local(wq_hbm.at[:, pl.ds(g * GCOLS, GCOLS)], wq_v.at[g]) for g in range(NGROUP)]
    ld_uv = local(wuv_hbm, wuv_v)
    ld_o = local(wo_hbm, wo_v)


    lane = lax.broadcasted_iota(jnp.int32, (TOK, 128), 1)
    low = lane < RD

    ld_kr.wait()
    for h in range(2):
        krp[0, h] = jnp.concatenate([ckr_v[2 * h], ckr_v[2 * h + 1]], axis=-1)

    def page_copies(name):
        sc, sh, tc, th, d = FLOWS[name]
        i = 2 * FLOW_ID[name]
        return [
            pltpu.make_async_remote_copy(src_ref=kc.at[sc, :, sh], dst_ref=kc.at[tc, :, th], send_sem=send_sem.at[i],
                                         recv_sem=recv_sem.at[i], device_id=(peer[d],), device_id_type=MESH),
            pltpu.make_async_remote_copy(src_ref=krp.at[sc, sh], dst_ref=krp.at[tc, th], send_sem=send_sem.at[i + 1],
                                         recv_sem=recv_sem.at[i + 1], device_id=(peer[d],), device_id_type=MESH),
        ]

    def new_copies(name):
        s, t, d, halves, tag = NEWS[name]
        rows = slice(halves[0], halves[-1] + 1)
        i = NEW_ID[(name, "c")]
        out = [pltpu.make_async_remote_copy(src_ref=nc.at[s, rows], dst_ref=nc.at[t, rows], send_sem=send_sem.at[i],
                                            recv_sem=recv_sem.at[i], device_id=(peer[d],), device_id_type=MESH)]
        if tag:
            i = NEW_ID[(name, "k")]
            out.append(pltpu.make_async_remote_copy(src_ref=nk.at[s], dst_ref=nk.at[t], send_sem=send_sem.at[i],
                                                    recv_sem=recv_sem.at[i], device_id=(peer[d],), device_id_type=MESH))
        return out

    started = []

    def send(name):
        for cp in (page_copies if name in FLOWS else new_copies)(name):
            cp.start()
            started.append(cp)

    def arrived(name):
        for cp in (page_copies if name in FLOWS else new_copies)(name):
            cp.wait_recv()

    with scope("barrier_send"):
        pl.semaphore_wait(barrier, 3)
        for cp in ld_c:
            cp.wait()
        for name in ("x0", "y1", "p0", "p1", "x1", "y0"):
            send(name)

    out_cps = [local(kc.at[0, p % 2, p // 2], cco_hbm.at[p]) for p in range(4)]
    out_cps.append(local(ckr_v.at[pl.ds(0, 4)], ckro_hbm.at[pl.ds(0, 4)]))

    with scope("tables"):
        for cp in ld_small:
            cp.wait()
        k_lane = lax.rem(lane, 32)
        freq = jnp.zeros((TOK, 128), F32)
        for k, f in enumerate(INV_FREQ):
            freq = jnp.where(k_lane == k, f, freq)
        pos = (lax.broadcasted_iota(jnp.int32, (TOK, 128), 0) + plen_s[0]).astype(F32)
        ang = pos * freq
        cos_t = jnp.cos(ang)
        sin_t = jnp.sin(ang)
        sin_t = jnp.where(lax.rem(lane, 64) < 32, -sin_t, sin_t)

    def rope2(v64):
        v = jnp.concatenate([v64, v64], axis=-1)
        return v * cos_t + pltpu.roll(v, 32, 1) * sin_t

    with scope("newlat"):
        ld_x.wait()
        ld_dkv.wait()
        kv = lax.dot_general(x_v[...], wdkv_v[...], (((1,), (1,)), ((), ())), preferred_element_type=F32)
        latp = kv[:, :LAT]
        inv_rms = lax.rsqrt(jnp.mean(latp * latp, axis=-1, keepdims=True) + EPS)
        c_new = (latp * inv_rms * g_v[...].astype(F32).reshape(1, LAT)).astype(BF)
        kr_dup = rope2(kv[:, LAT:]).astype(BF)
        nc[0, 0] = c_new[:32]
        nc[0, 1] = c_new[32:]
        nk[0, pl.ds(0, 32)] = jnp.where(low[:32], kr_dup[:32], kr_dup[32:])
        nk[0, pl.ds(32, 16)] = jnp.full((16, 128), wt_s[0, 0], jnp.int32).astype(F32).astype(BF)

    with scope("mult"):
        tbl = tbl_v[...]
        ids = (tbl[0:1] * 4 + tbl[1:2]).astype(F32)
        ids_col = jnp.transpose(jnp.broadcast_to(ids, (128, 256)))
        seg = lax.div(lax.broadcasted_iota(jnp.int32, (1, 256), 1), 64)
        flips = {0: 0, 1: fp, 2: fx, 4: fy, 3: fp + fx, 5: fp + fy, 6: fx + fy, 7: fp + fx + fy}
        for c, ((ra, ha), (rb, hb)) in enumerate(CHUNKS):
            pa = (me + flips[ra]) * 4 + 2 * ha
            pb = (me + flips[rb]) * 4 + 2 * hb
            want = jnp.where(seg == 0, pa, jnp.where(seg == 1, pb, jnp.where(seg == 2, pa + 1, pb + 1))).astype(F32)
            parts = []
            for t in range(2):
                hit = jnp.where(ids_col == want[:, t * 128:(t + 1) * 128], 1.0, 0.0)
                parts.append(jnp.sum(hit, axis=0, keepdims=True))
            cnt = jnp.concatenate(parts, axis=-1)
            bias_s[c] = jnp.where(cnt > 0.0, jnp.log2(jnp.maximum(cnt, 1.0)), -jnp.inf)

    r_i = lax.broadcasted_iota(jnp.int32, (256, 256), 0)
    c_i = lax.broadcasted_iota(jnp.int32, (256, 256), 1)
    perm = (r_i == lax.rem(c_i, 16) * 16 + lax.div(c_i, 16)).astype(F32).astype(BF)

    def reorder(src, dst):
        def step(i, carry):
            for u in range(4):
                blk = i * 8 + 2 * u
                rows = [src[pl.ds(pl.multiple_of((blk + v) * 256, 256), 256), :] for v in range(2)]
                t = jnp.dot(perm, jnp.concatenate(rows, axis=-1), preferred_element_type=F32).astype(BF)
                for v in range(2):
                    dst[:, pl.ds(pl.multiple_of((blk + v) * 16, 16), 16), :] = t[:, v * 128:(v + 1) * 128].reshape(NH, 16, 128)
            return carry
        lax.fori_loop(0, 4, step, 0)

    with scope("reorder_uk"):
        ld_uk.wait()
        reorder(wuk_v, wukt)

    for g in range(NGROUP):
        with scope(f"waitq{g}"):
            ld_q[g].wait()
        with scope(f"query{g}"):
            qg = jnp.dot(x_v[...], wq_v[g], preferred_element_type=F32).astype(BF).astype(F32)
            for k in range(GROUP):
                h = g * GROUP + k
                nope = qg[:, k * HQ:k * HQ + ND].astype(BF)
                qr_s[pl.ds(h * TOK, TOK), :] = rope2(qg[:, k * HQ + ND:(k + 1) * HQ]).astype(BF)
                q_s[pl.ds(h * TOK, TOK), :] = lax.dot_general(
                    nope, wukt[h], (((1,), (1,)), ((), ())), preferred_element_type=F32).astype(BF)

    NT = (((1,), (1,)), ((), ()))
    row_tok = lax.rem(lax.broadcasted_iota(jnp.int32, (BLK, TOK), 0), TOK)
    causal = lax.broadcasted_iota(jnp.int32, (BLK, TOK), 1) <= row_tok
    lane2 = lax.broadcasted_iota(jnp.int32, (128, 128), 1)
    kr_low = jnp.where(low, kr_dup.astype(F32), 0.0).astype(BF)

    def rope_keys(c):
        if c < 0:
            return kr_low
        kp = krp[c].reshape(128, 128).astype(F32)
        return jnp.concatenate([jnp.where(lane2 < RD, kp, 0.0), jnp.where(lane2 < RD, 0.0, kp)], axis=0).astype(BF)

    def keys_of(c):
        return nc[0].reshape(TOK, LAT) if c < 0 else kc[c].reshape(256, LAT)

    def scores(c, b, slot, kbd):
        rows = pl.ds(b * BLK, BLK)
        s = lax.dot_general(q_s[rows, :], keys_of(c), NT, preferred_element_type=F32)
        s = s + lax.dot_general(qr_s[rows, :], kbd, NT, preferred_element_type=F32)
        if c < 0:
            s_s[slot, :, :TOK] = s
        else:
            s_s[slot] = s

    def accumulate(c, b, slot):
        rows = pl.ds(b * BLK, BLK)
        if c < 0:
            t = jnp.where(causal, s_s[slot, :, :TOK] * SCALE2, -jnp.inf)
            mx = jnp.max(t, axis=-1, keepdims=True)
            p = jnp.exp2(t - mx)
            m_s[rows, :] = jnp.broadcast_to(mx, (BLK, 128))
            l_s[rows, :] = jnp.concatenate([p, jnp.zeros_like(p)], axis=-1)
            o_s[rows, :] = jnp.dot(p.astype(BF), keys_of(c), preferred_element_type=F32)
            return
        bias = bias_s[c]
        t = s_s[slot] * SCALE2 + bias
        mx = jnp.max(jnp.maximum(t[:, :128], t[:, 128:]), axis=-1, keepdims=True)
        m_old = m_s[rows, :]
        m_new = jnp.maximum(m_old, jnp.broadcast_to(mx, (BLK, 128)))
        alpha = jnp.exp2(m_old - m_new)
        p = jnp.exp2(t - jnp.concatenate([m_new, m_new], axis=-1))
        m_s[rows, :] = m_new
        l_s[rows, :] = l_s[rows, :] * alpha + (p[:, :128] + p[:, 128:])
        a4 = jnp.concatenate([alpha] * 4, axis=-1)
        o_s[rows, :] = o_s[rows, :] * a4 + jnp.dot(p.astype(BF), keys_of(c), preferred_element_type=F32)

    def arrive(*names):
        with scope("wait_" + names[0]):
            for name in names:
                arrived(name)

    def sends(*names):
        for name in names:
            send(name)

    def before(c):
        if c == 0:
            arrive("x0", "y1")
            sends("dy", "dx", "p20", "p21", "nx", "ny", "np")
        elif c == 1:
            arrive("p0", "p1")
        elif c == 3:
            arrive("p20", "p21")
        elif c == 4:
            arrive("x1", "y0")
            sends("p40", "p41")
        elif c == 5:
            arrive("p40", "p41")
        elif c == 6:
            arrive("dy", "dx")
            sends("p60", "p61")
            arrive("nx", "ny")
            sends("ndy", "ndx", "n2p", "n4p")
        elif c == 7:
            arrive("p60", "p61")

    nblk = ROWS // BLK
    prev = None
    for c in (-1, 0, 1, 2, 4, 3, 5, 6, 7):
        before(c)
        if c == 4:
            with scope("reorder_uv"):
                ld_uv.wait()
                reorder(wuv_v, wuvt)
        with scope(f"attend{c}"):
            kbd = rope_keys(c)
            for b in range(nblk):
                scores(c, b, b % 2, kbd)
                if prev is not None:
                    accumulate(*prev)
                prev = (c, b, b % 2)
    with scope("attend_last"):
        accumulate(*prev)

    with scope("values"):
        for h in range(NH):
            rows = pl.ds(h * TOK, TOK)
            denom = jnp.sum(l_s[rows, :], axis=-1, keepdims=True)
            ol = (o_s[rows, :] / denom).astype(BF)
            ob_s[:, pl.ds(h * ND, ND)] = jnp.dot(ol, wuvt[h], preferred_element_type=F32).astype(BF)
    with scope("wait_ndy"):
        for name in ("ndy", "ndx"):
            arrived(name)
    send("n6p")
    with scope("wait_wo"):
        ld_o.wait()
    NB = 512

    def out_step(j, carry):
        cols = pl.ds(pl.multiple_of(j * NB, NB), NB)
        acc = jnp.dot(ob_s[...], wo_v[:, cols], preferred_element_type=F32)
        y_v[:, cols] = (x_v[:, cols].astype(F32) + acc).astype(BF)
        return carry
    with scope("outproj"):
        lax.fori_loop(0, DM // NB, out_step, 0)
    y_cp = local(y_v, y_hbm)

    with scope("wait_np"):
        for name in ("np", "n2p", "n4p", "n6p"):
            arrived(name)
    with scope("page"):
        mine = me.astype(F32)
        pc = [jnp.zeros((32, LAT), F32) for _ in range(2)]
        pk = jnp.zeros((32, 128), F32)
        for r in range(8):
            hit = nk[r, pl.ds(32, 16)].astype(F32)
            hit = jnp.concatenate([hit, hit], axis=0) == mine
            pk = jnp.where(hit, nk[r, pl.ds(0, 32)].astype(F32), pk)
            hit4 = jnp.concatenate([hit] * 4, axis=-1)
            for u in range(2):
                pc[u] = jnp.where(hit4, nc[r, u].astype(F32), pc[u])
        pc_v[pl.ds(0, 32), :] = pc[0].astype(BF)
        pc_v[pl.ds(32, 32), :] = pc[1].astype(BF)
        pkb = pk.astype(BF)
        pk_v[pl.ds(0, 32), :] = pkb[:, :RD]
        pk_v[pl.ds(32, 32), :] = pkb[:, RD:]
        out_cps.append(local(pc_v, cco_hbm.at[4]))
        out_cps.append(local(pk_v, ckro_hbm.at[4]))
    with scope("final_wait"):
        for cp in started:
            cp.wait_send()
        y_cp.wait()
        for cp in out_cps:
            cp.wait()


def fused(x, plen, tbl, wt, cc, ckr, wq, wdkv, g, wuk, wuv, wo):
    any_spec = pl.BlockSpec(memory_space=pl.ANY)
    dma = pltpu.SemaphoreType.DMA
    return pl.pallas_call(
        body,
        name="mla_prefill",
        out_shape=(
            jax.ShapeDtypeStruct((TOK, DM), BF),
            jax.ShapeDtypeStruct((5, TOK, LAT), BF),
            jax.ShapeDtypeStruct((5, TOK, RD), BF),
        ),
        in_specs=[any_spec] * 12,
        out_specs=(any_spec,) * 3,
        scratch_shapes=[
            pltpu.VMEM((TOK, DM), BF),
            pltpu.SMEM((1,), jnp.int32),
            pltpu.VMEM((2, 256), jnp.int32),
            pltpu.SMEM((1, 2), jnp.int32),
            pltpu.VMEM((5, TOK, RD), BF),
            pltpu.VMEM((NGROUP, DM, GCOLS), BF),
            pltpu.VMEM((LAT + RD, DM), BF),
            pltpu.VMEM((LAT,), BF),
            pltpu.VMEM((LAT * NH, ND), BF),
            pltpu.VMEM((LAT * NH, ND), BF),
            pltpu.VMEM((DM, DM), BF),
            pltpu.VMEM((8, 2, 2, TOK, LAT), BF),
            pltpu.VMEM((8, 2, TOK, 128), BF),
            pltpu.VMEM((8, 2, 32, LAT), BF),
            pltpu.VMEM((8, 48, 128), BF),
            pltpu.VMEM((NH, LAT, ND), BF),
            pltpu.VMEM((NH, LAT, ND), BF),
            pltpu.VMEM((ROWS, LAT), BF),
            pltpu.VMEM((ROWS, 128), BF),
            pltpu.VMEM((2, BLK, 256), F32),
            pltpu.VMEM((ROWS, LAT), F32),
            pltpu.VMEM((ROWS, 128), F32),
            pltpu.VMEM((ROWS, 128), F32),
            pltpu.VMEM((8, 1, 256), F32),
            pltpu.VMEM((TOK, DM), BF),
            pltpu.VMEM((TOK, DM), BF),
            pltpu.VMEM((TOK, LAT), BF),
            pltpu.VMEM((TOK, RD), BF),
            dma((32,)),
            dma((NSEM,)),
            dma((NSEM,)),
        ],
        compiler_params=pltpu.CompilerParams(collective_id=0, has_side_effects=True, vmem_limit_bytes=60 * 1024 * 1024),
    )(x, plen, tbl, wt, cc, ckr, wq, wdkv, g, wuk, wuv, wo)


def solution(mesh):
    def device_step(hidden, pre_len, pre_table, wr_table, cache_c, cache_kr, w_q, w_dkv, g_kv, w_uk, w_uv, w_o):
        y, c_out, kr_out = fused(
            hidden.reshape(TOK, DM), pre_len, pre_table.reshape(256, 2).T, wr_table.reshape(1, 2), cache_c[0], cache_kr[0],
            w_q, w_dkv.T, g_kv, w_uk.reshape(LAT * NH, ND), w_uv.reshape(LAT * NH, ND), w_o)
        return y[None], c_out[None], kr_out[None]

    row = P("pool")
    rep = P()
    return jax.shard_map(device_step, mesh=mesh, in_specs=(row,) * 6 + (rep,) * 6, out_specs=(row, row, row), check_vma=False)
```

time: 43.2 us -> 32.7 us (0.76)
  Pallas kernels: 35.5 us -> 26.3 us
  local copies, waits for them, and re-layouts: 6.18 us -> 4.92 us
    pallas_call x1, Pallas kernels: 35.5 us -> 26.3 us  [fused(): pl.pallas_call(body, name='mla_prefill', out_shape=(jax.ShapeDtypeStruct(...]
    reshape x1 -> x0, local copies, waits for them, and re-layouts: 1.26 us -> none  [device_step(): g_kv.reshape(1, LAT)]
where the time goes in v2:
time: 32.7 us; the launch traced here: 32.5 us
  Pallas kernels  26.3 us (80%)
  local copies, waits for them, and re-layouts  4.92 us (15%)
  between operations  1.29 us (4%)
    pallas_call x1, Pallas kernels, fused(): pl.pallas_call(body, name='mla_prefill', out_shape=(jax.ShapeDtypeStruct(...  26.3 us
    unnamed x3, local copies, waits for them, and re-layouts  4.92 us

profile of v2, /device:TPU:0, one launch (start us, length us, event | category | flops | bytes accessed | tf_op | source)
XLA Modules:
  0.0 32.5 jit_solution(5130924971718700178)
XLA Ops:
  1.3 26.3 %mla_prefill.1 = (bf16[64,2048]{1,0:T(8,128)(2,1)}, bf16[5,64,512]{2,1,0:T(8,128)(2,1)}, bf16[5,64,64]{2,1,0:T(8,128)(2,1)}) custom-call(bf16[64,2048]{1,0:T(8,128)(2,1)} %bitcast.18, s32[1]{0:T(128)S(6)} %copy.18.plen_hbm, s32[2,256]{1,0:T(2,128)} %bitcast.22, s32[1,2]{1,0:T(1,128)} %bitcast.23, bf16[5,64,512]{2,1,0:T(8,128)(2,1)} %bitcast.17, ...), custom_call_target="tpu_custom_call" | custom-call | tf_op jit(solution)/shard_map/mla_prefill/pallas_call | solution.py:399
  27.6 1.7 %copy.19 = bf16[1,64,2048]{2,1,0:T(8,128)(2,1)} copy(bf16[1,64,2048]{2,1,0:T(8,128)(2,1)} %bitcast.19) | data formatting | bytes 524288
  29.3 1.7 %copy.20 = bf16[1,5,64,512]{3,2,1,0:T(8,128)(2,1)} copy(bf16[1,5,64,512]{3,2,1,0:T(8,128)(2,1)} %bitcast.16) | data formatting | bytes 655360
  31.0 1.5 %copy.21 = bf16[1,5,64,64]{3,2,1,0:T(8,128)(2,1)} copy(bf16[1,5,64,64]{3,2,1,0:T(8,128)(2,1)} %bitcast.21) | data formatting | bytes 81920

commit v3 on v2

--- a/solution.py
+++ b/solution.py
@@ -82,10 +82,10 @@
     return jax.named_scope(name) if PROF else contextlib.nullcontext()
 
 
-def body(x_hbm, plen_hbm, tbl_hbm, wt_hbm, cc_hbm, ckr_hbm, wq_hbm, wdkv_hbm, g_hbm, wuk_hbm, wuv_hbm, wo_hbm,
-         y_hbm, cco_hbm, ckro_hbm,
-         x_v, plen_s, tbl_v, wt_s, ckr_v, wq_v, wdkv_v, g_v, wuk_v, wuv_v, wo_v,
-         kc, krp, nc, nk, wukt, wuvt, q_s, qr_s, s_s, o_s, m_s, l_s, bias_s, ob_s, y_v, pc_v, pk_v,
+def body(x_hbm, tbl_hbm, wt_hbm, cc_hbm, ckr_hbm, wq_hbm, wdkv_hbm, g_hbm, wuk_hbm, wuv_hbm,
+         ob_hbm, pc_hbm, pk_hbm,
+         x_v, tbl_v, wt_s, ckr_v, wq_v, wdkv_v, g_v, wuk_v, wuv_v,
+         kc, krp, nc, nk, wukt, wuvt, q_s, qn_s, qr_s, s_s, o_s, m_s, l_s, bias_s, ob_s, pc_v, pk_v,
          loc_sem, send_sem, recv_sem):
     me = lax.axis_index("pool")
     core = lax.rem(me, 2)
@@ -112,11 +112,10 @@
     ld_c = [local(cc_hbm.at[p], kc.at[0, p % 2, p // 2]) for p in range(4)]
     ld_x = local(x_hbm, x_v)
     ld_dkv = local(wdkv_hbm, wdkv_v)
-    ld_small = [local(plen_hbm, plen_s), local(tbl_hbm, tbl_v), local(wt_hbm, wt_s), local(g_hbm, g_v)]
+    ld_small = [local(tbl_hbm, tbl_v), local(wt_hbm, wt_s), local(g_hbm, g_v)]
     ld_uk = local(wuk_hbm, wuk_v)
     ld_q = [local(wq_hbm.at[:, pl.ds(g * GCOLS, GCOLS)], wq_v.at[g]) for g in range(NGROUP)]
     ld_uv = local(wuv_hbm, wuv_v)
-    ld_o = local(wo_hbm, wo_v)
 
 
     lane = lax.broadcasted_iota(jnp.int32, (TOK, 128), 1)
@@ -159,15 +158,13 @@
         for cp in (page_copies if name in FLOWS else new_copies)(name):
             cp.wait_recv()
 
-    with scope("barrier_send"):
+    with scope("barrier"):
         pl.semaphore_wait(barrier, 3)
+    with scope("send0"):
         for cp in ld_c:
             cp.wait()
         for name in ("x0", "y1", "p0", "p1", "x1", "y0"):
             send(name)
-
-    out_cps = [local(kc.at[0, p % 2, p // 2], cco_hbm.at[p]) for p in range(4)]
-    out_cps.append(local(ckr_v.at[pl.ds(0, 4)], ckro_hbm.at[pl.ds(0, 4)]))
 
     with scope("tables"):
         for cp in ld_small:
@@ -176,7 +173,8 @@
         freq = jnp.zeros((TOK, 128), F32)
         for k, f in enumerate(INV_FREQ):
             freq = jnp.where(k_lane == k, f, freq)
-        pos = (lax.broadcasted_iota(jnp.int32, (TOK, 128), 0) + plen_s[0]).astype(F32)
+        n_pages = jnp.sum(jnp.where(tbl_v[0:1] >= 0, 1.0, 0.0), axis=-1, keepdims=True)
+        pos = lax.broadcasted_iota(jnp.int32, (TOK, 128), 0).astype(F32) + jnp.broadcast_to(n_pages * TOK, (TOK, 128))
         ang = pos * freq
         cos_t = jnp.cos(ang)
         sin_t = jnp.sin(ang)
@@ -221,31 +219,33 @@
     perm = (r_i == lax.rem(c_i, 16) * 16 + lax.div(c_i, 16)).astype(F32).astype(BF)
 
     def reorder(src, dst):
-        def step(i, carry):
-            for u in range(4):
-                blk = i * 8 + 2 * u
-                rows = [src[pl.ds(pl.multiple_of((blk + v) * 256, 256), 256), :] for v in range(2)]
-                t = jnp.dot(perm, jnp.concatenate(rows, axis=-1), preferred_element_type=F32).astype(BF)
-                for v in range(2):
-                    dst[:, pl.ds(pl.multiple_of((blk + v) * 16, 16), 16), :] = t[:, v * 128:(v + 1) * 128].reshape(NH, 16, 128)
-            return carry
-        lax.fori_loop(0, 4, step, 0)
+        for blk in range(0, 32, 2):
+            rows = jnp.concatenate([src[pl.ds((blk + v) * 256, 256), :] for v in range(2)], axis=-1)
+            t = jnp.dot(perm, rows, preferred_element_type=F32).astype(BF)
+            for v in range(2):
+                dst[:, pl.ds((blk + v) * 16, 16), :] = t[:, v * 128:(v + 1) * 128].reshape(NH, 16, 128)
 
     with scope("reorder_uk"):
         ld_uk.wait()
         reorder(wuk_v, wukt)
+
+    def lift(g):
+        for k in range(GROUP):
+            h = g * GROUP + k
+            q_s[pl.ds(h * TOK, TOK), :] = lax.dot_general(
+                qn_s[h], wukt[h], (((1,), (1,)), ((), ())), preferred_element_type=F32).astype(BF)
 
     for g in range(NGROUP):
         with scope(f"waitq{g}"):
             ld_q[g].wait()
         with scope(f"query{g}"):
             qg = jnp.dot(x_v[...], wq_v[g], preferred_element_type=F32).astype(BF).astype(F32)
+            if g:
+                lift(g - 1)
             for k in range(GROUP):
                 h = g * GROUP + k
-                nope = qg[:, k * HQ:k * HQ + ND].astype(BF)
+                qn_s[h] = qg[:, k * HQ:k * HQ + ND].astype(BF)
                 qr_s[pl.ds(h * TOK, TOK), :] = rope2(qg[:, k * HQ + ND:(k + 1) * HQ]).astype(BF)
-                q_s[pl.ds(h * TOK, TOK), :] = lax.dot_general(
-                    nope, wukt[h], (((1,), (1,)), ((), ())), preferred_element_type=F32).astype(BF)
 
     NT = (((1,), (1,)), ((), ()))
     row_tok = lax.rem(lax.broadcasted_iota(jnp.int32, (BLK, TOK), 0), TOK)
@@ -335,7 +335,9 @@
             kbd = rope_keys(c)
             for b in range(nblk):
                 scores(c, b, b % 2, kbd)
-                if prev is not None:
+                if prev is None:
+                    lift(NGROUP - 1)
+                else:
                     accumulate(*prev)
                 prev = (c, b, b % 2)
     with scope("attend_last"):
@@ -347,26 +349,11 @@
             denom = jnp.sum(l_s[rows, :], axis=-1, keepdims=True)
             ol = (o_s[rows, :] / denom).astype(BF)
             ob_s[:, pl.ds(h * ND, ND)] = jnp.dot(ol, wuvt[h], preferred_element_type=F32).astype(BF)
-    with scope("wait_ndy"):
-        for name in ("ndy", "ndx"):
-            arrived(name)
+    arrive("ndy", "ndx")
     send("n6p")
-    with scope("wait_wo"):
-        ld_o.wait()
-    NB = 512
-
-    def out_step(j, carry):
-        cols = pl.ds(pl.multiple_of(j * NB, NB), NB)
-        acc = jnp.dot(ob_s[...], wo_v[:, cols], preferred_element_type=F32)
-        y_v[:, cols] = (x_v[:, cols].astype(F32) + acc).astype(BF)
-        return carry
-    with scope("outproj"):
-        lax.fori_loop(0, DM // NB, out_step, 0)
-    y_cp = local(y_v, y_hbm)
-
-    with scope("wait_np"):
-        for name in ("np", "n2p", "n4p", "n6p"):
-            arrived(name)
+    ob_cp = local(ob_s, ob_hbm)
+
+    arrive("np", "n2p", "n4p", "n6p")
     with scope("page"):
         mine = me.astype(F32)
         pc = [jnp.zeros((32, LAT), F32) for _ in range(2)]
@@ -383,17 +370,63 @@
         pkb = pk.astype(BF)
         pk_v[pl.ds(0, 32), :] = pkb[:, :RD]
         pk_v[pl.ds(32, 32), :] = pkb[:, RD:]
-        out_cps.append(local(pc_v, cco_hbm.at[4]))
-        out_cps.append(local(pk_v, ckro_hbm.at[4]))
+        pc_cp = local(pc_v, pc_hbm)
+        pk_cp = local(pk_v, pk_hbm)
     with scope("final_wait"):
         for cp in started:
             cp.wait_send()
-        y_cp.wait()
-        for cp in out_cps:
-            cp.wait()
-
-
-def fused(x, plen, tbl, wt, cc, ckr, wq, wdkv, g, wuk, wuv, wo):
+        ob_cp.wait()
+        pc_cp.wait()
+        pk_cp.wait()
+
+
+def finish_body(x_v, ob_v, wo_v, cc_v, ckr_v, pc_v, pk_v, y_hbm, cco_hbm, ckro_hbm, y_v, sem):
+    n = [0]
+
+    def local(src, dst):
+        cp = pltpu.make_async_copy(src, dst, sem.at[n[0]])
+        n[0] += 1
+        cp.start()
+        return cp
+
+    NB = 512
+    outs = [
+        local(cc_v.at[pl.ds(0, 4)], cco_hbm.at[pl.ds(0, 4)]),
+        local(ckr_v.at[pl.ds(0, 4)], ckro_hbm.at[pl.ds(0, 4)]),
+        local(pc_v, cco_hbm.at[4]),
+        local(pk_v, ckro_hbm.at[4]),
+    ]
+    for j in range(DM // NB):
+        cols = pl.ds(j * NB, NB)
+        acc = jnp.dot(ob_v[...], wo_v[:, cols], preferred_element_type=F32)
+        y_v[:, cols] = (x_v[:, cols].astype(F32) + acc).astype(BF)
+        outs.append(local(y_v.at[:, cols], y_hbm.at[:, cols]))
+    for cp in outs:
+        cp.wait()
+
+
+def finish(x, ob, wo, cc, ckr, pc, pk):
+    any_spec = pl.BlockSpec(memory_space=pl.ANY)
+    vm = pl.BlockSpec(memory_space=pltpu.VMEM)
+    return pl.pallas_call(
+        finish_body,
+        name="mla_finish",
+        out_shape=(
+            jax.ShapeDtypeStruct((TOK, DM), BF),
+            jax.ShapeDtypeStruct((5, TOK, LAT), BF),
+            jax.ShapeDtypeStruct((5, TOK, RD), BF),
+        ),
+        in_specs=[vm] * 7,
+        out_specs=(any_spec,) * 3,
+        scratch_shapes=[
+            pltpu.VMEM((TOK, DM), BF),
+            pltpu.SemaphoreType.DMA((8,)),
+        ],
+        compiler_params=pltpu.CompilerParams(vmem_limit_bytes=16 * 1024 * 1024),
+    )(x, ob, wo, cc, ckr, pc, pk)
+
+
+def fused(x, tbl, wt, cc, ckr, wq, wdkv, g, wuk, wuv):
     any_spec = pl.BlockSpec(memory_space=pl.ANY)
     dma = pltpu.SemaphoreType.DMA
     return pl.pallas_call(
@@ -401,14 +434,13 @@
         name="mla_prefill",
         out_shape=(
             jax.ShapeDtypeStruct((TOK, DM), BF),
-            jax.ShapeDtypeStruct((5, TOK, LAT), BF),
-            jax.ShapeDtypeStruct((5, TOK, RD), BF),
+            jax.ShapeDtypeStruct((TOK, LAT), BF),
+            jax.ShapeDtypeStruct((TOK, RD), BF),
         ),
-        in_specs=[any_spec] * 12,
+        in_specs=[pl.BlockSpec(memory_space=pltpu.HBM)] * 10,
         out_specs=(any_spec,) * 3,
         scratch_shapes=[
             pltpu.VMEM((TOK, DM), BF),
-            pltpu.SMEM((1,), jnp.int32),
             pltpu.VMEM((2, 256), jnp.int32),
             pltpu.SMEM((1, 2), jnp.int32),
             pltpu.VMEM((5, TOK, RD), BF),
@@ -417,7 +449,6 @@
             pltpu.VMEM((LAT,), BF),
             pltpu.VMEM((LAT * NH, ND), BF),
             pltpu.VMEM((LAT * NH, ND), BF),
-            pltpu.VMEM((DM, DM), BF),
             pltpu.VMEM((8, 2, 2, TOK, LAT), BF),
             pltpu.VMEM((8, 2, TOK, 128), BF),
             pltpu.VMEM((8, 2, 32, LAT), BF),
@@ -425,6 +456,7 @@
             pltpu.VMEM((NH, LAT, ND), BF),
             pltpu.VMEM((NH, LAT, ND), BF),
             pltpu.VMEM((ROWS, LAT), BF),
+            pltpu.VMEM((NH, TOK, ND), BF),
             pltpu.VMEM((ROWS, 128), BF),
             pltpu.VMEM((2, BLK, 256), F32),
             pltpu.VMEM((ROWS, LAT), F32),
@@ -432,22 +464,23 @@
             pltpu.VMEM((ROWS, 128), F32),
             pltpu.VMEM((8, 1, 256), F32),
             pltpu.VMEM((TOK, DM), BF),
-            pltpu.VMEM((TOK, DM), BF),
             pltpu.VMEM((TOK, LAT), BF),
             pltpu.VMEM((TOK, RD), BF),
             dma((32,)),
             dma((NSEM,)),
             dma((NSEM,)),
         ],
-        compiler_params=pltpu.CompilerParams(collective_id=0, has_side_effects=True, vmem_limit_bytes=60 * 1024 * 1024),
-    )(x, plen, tbl, wt, cc, ckr, wq, wdkv, g, wuk, wuv, wo)
+        compiler_params=pltpu.CompilerParams(collective_id=0, has_side_effects=True, vmem_limit_bytes=40 * 1024 * 1024),
+    )(*[pltpu.with_memory_space_constraint(a, pltpu.HBM) for a in (x, tbl, wt, cc, ckr, wq, wdkv, g, wuk, wuv)])
 
 
 def solution(mesh):
     def device_step(hidden, pre_len, pre_table, wr_table, cache_c, cache_kr, w_q, w_dkv, g_kv, w_uk, w_uv, w_o):
-        y, c_out, kr_out = fused(
-            hidden.reshape(TOK, DM), pre_len, pre_table.reshape(256, 2).T, wr_table.reshape(1, 2), cache_c[0], cache_kr[0],
-            w_q, w_dkv.T, g_kv, w_uk.reshape(LAT * NH, ND), w_uv.reshape(LAT * NH, ND), w_o)
+        x = hidden.reshape(TOK, DM)
+        ob, pc, pk = fused(
+            x, pre_table.reshape(256, 2).T, wr_table.reshape(1, 2), cache_c[0], cache_kr[0],
+            w_q, w_dkv.T, g_kv, w_uk.reshape(LAT * NH, ND), w_uv.reshape(LAT * NH, ND))
+        y, c_out, kr_out = finish(x, ob, w_o, cache_c[0], cache_kr[0], pc, pk)
         return y[None], c_out[None], kr_out[None]
 
     row = P("pool")

time: 32.7 us -> 26.6 us (0.81)
  local copies, waits for them, and re-layouts: 4.92 us -> 0.02 us
  Pallas kernels: 26.3 us -> 25.6 us
  between operations: 1.29 us -> 0.89 us
    unnamed x3 -> x10, local copies, waits for them, and re-layouts: 4.92 us -> 0.02 us
    pallas_call x1, Pallas kernels: 26.3 us -> 23.3 us  [fused(): pl.pallas_call(body, name='mla_prefill', out_shape=(jax.ShapeDtypeStruct(...]
    pallas_call x0 -> x1, Pallas kernels: none -> 2.28 us  [finish(): pl.pallas_call(finish_body, name='mla_finish', out_shape=(jax.ShapeDtypeS...]
where the time goes in v3:
time: 26.6 us; the launch traced here: 26.5 us
  Pallas kernels  25.6 us (96%)
  between operations  0.89 us (3%)
    pallas_call x1, Pallas kernels, fused(): pl.pallas_call(body, name='mla_prefill', out_shape=(jax.ShapeDtypeStruct(...  23.3 us
    pallas_call x1, Pallas kernels, finish(): pl.pallas_call(finish_body, name='mla_finish', out_shape=(jax.ShapeDtypeS...  2.28 us

profile of v3, /device:TPU:0, one launch (start us, length us, event | category | flops | bytes accessed | tf_op | source)
XLA Modules:
  0.0 26.5 jit_solution(7403003074871689017)
XLA Ops:
  0.6 0.0 slice-start
  0.6 0.0 slice-start.1
  0.7 0.0 copy-start
  0.7 0.0 copy-start.1
  0.7 0.0 copy-start.2
  0.7 23.3 %mla_prefill.1 = (bf16[64,2048]{1,0:T(8,128)(2,1)S(1)}, bf16[64,512]{1,0:T(8,128)(2,1)S(1)}, bf16[64,64]{1,0:T(8,128)(2,1)S(1)}) custom-call(bf16[64,2048]{1,0:T(8,128)(2,1)} %bitcast.17, s32[2,256]{1,0:T(2,128)} %bitcast.24, s32[1,2]{1,0:T(1,128)} %bitcast.25, bf16[5,64,512]{2,1,0:T(8,128)(2,1)} %bitcast.15, bf16[5,64,64]{2,1,0:T(8,128)(2,1)} %bitcast.19, ...), custom_call_target="tpu_custom_call" | custom-call | tf_op jit(solution)/shard_map/mla_prefill/pallas_call | solution.py:432
  24.0 0.0 slice-done
  24.0 0.0 slice-done.1
  24.0 0.0 copy-done
  24.0 0.0 copy-done.1
  24.0 0.0 copy-done.2
  24.0 2.3 %mla_finish.1 = (bf16[64,2048]{1,0:T(8,128)(2,1)}, bf16[5,64,512]{2,1,0:T(8,128)(2,1)}, bf16[5,64,64]{2,1,0:T(8,128)(2,1)}) custom-call(bf16[64,2048]{1,0:T(8,128)(2,1)S(1)} %bitcast.18, bf16[64,2048]{1,0:T(8,128)(2,1)S(1)} %get-tuple-element.9.ob_v, bf16[2048,2048]{1,0:T(8,128)(2,1)S(1)} %bitcast.14, bf16[5,64,512]{2,1,0:T(8,128)(2,1)S(1)} %bitcast.16, ...), custom_call_target="tpu_custom_call" | custom-call | tf_op jit(solution)/shard_map/mla_finish/pallas_call | solution.py:411
  (1 shorter events, 0.0 us)
Async XLA Ops:
  0.6 23.3 %slice-start = ((s8[8388608]{0:T(1024)(128)(4,1)}), s8[4194304]{0:T(1024)(128)(4,1)S(1)}, s32[]{:S(2)}) async-start(s8[8388608]{0:T(1024)(128)(4,1)} %bitcast.13), calls=%async_computation | async-start | bytes 8388608
  0.6 23.3 %slice-start.1 = ((s8[8388608]{0:T(1024)(128)(4,1)}), s8[4194304]{0:T(1024)(128)(4,1)S(1)}, s32[]{:S(2)}) async-start(s8[8388608]{0:T(1024)(128)(4,1)} %bitcast.13), calls=%async_computation.1 | async-start | bytes 8388608
  0.7 23.3 %copy-start = (bf16[1,5,64,512]{3,2,1,0:T(8,128)(2,1)S(1)}, bf16[1,5,64,512]{3,2,1,0:T(8,128)(2,1)}, u32[]{:S(2)}) copy-start(bf16[1,5,64,512]{3,2,1,0:T(8,128)(2,1)} %param.15) | copy-start | bytes 983044
  0.7 23.3 %copy-start.1 = (bf16[1,64,2048]{2,1,0:T(8,128)(2,1)S(1)}, bf16[1,64,2048]{2,1,0:T(8,128)(2,1)}, u32[]{:S(2)}) copy-start(bf16[1,64,2048]{2,1,0:T(8,128)(2,1)} %param.12) | copy-start | bytes 786436
  0.7 23.3 %copy-start.2 = (bf16[1,5,64,64]{3,2,1,0:T(8,128)(2,1)S(1)}, bf16[1,5,64,64]{3,2,1,0:T(8,128)(2,1)}, u32[]{:S(2)}) copy-start(bf16[1,5,64,64]{3,2,1,0:T(8,128)(2,1)} %param.16) | copy-start | bytes 122884

commit v4 on v3

v4 whole, which is shorter than its diff:
```python
import contextlib
import math

import jax
import jax.numpy as jnp
import numpy as np
from jax import lax
from jax.experimental import pallas as pl
from jax.experimental.pallas import tpu as pltpu
from jax.sharding import PartitionSpec as P

BF = jnp.bfloat16
PROF = False
F32 = jnp.float32
MESH = pl.DeviceIdType.MESH

TOK = 64
DM = 2048
NH = 16
LAT = 512
RD = 64
ND = 128
HQ = ND + RD
ROWS = NH * TOK
EPS = 1e-6
GROUP = 4
GCOLS = GROUP * HQ
NB = 512
NGROUP = NH // GROUP
BLK = 256
SCALE2 = float((ND + RD) ** -0.5 * math.log2(math.e))
INV_FREQ = [float(np.float32(10000.0 ** (-k / 32.0))) for k in range(32)]

CHUNKS = (
    ((0, 0), (0, 1)),
    ((1, 0), (1, 1)),
    ((2, 0), (4, 1)),
    ((3, 0), (5, 1)),
    ((2, 1), (4, 0)),
    ((3, 1), (5, 0)),
    ((6, 0), (6, 1)),
    ((7, 0), (7, 1)),
)
HALF = 128 + 16
NEWR = TOK + 16

FLOWS = {
    "x0": (0, 0, 2, 0, "x"),
    "x1": (0, 1, 4, 0, "x"),
    "y1": (0, 1, 2, 1, "y"),
    "y0": (0, 0, 4, 1, "y"),
    "p0": (0, None, 1, None, "p"),
    "dy": (2, 0, 6, 0, "y"),
    "dx": (2, 1, 6, 1, "x"),
    "p2": (2, None, 3, None, "p"),
    "p4": (4, None, 5, None, "p"),
    "p6": (6, None, 7, None, "p"),
}
NEWS = {
    "nx": (0, 1, "x", 8),
    "ny": (0, 2, "y", 8),
    "nd": (0, 3, "d", 8),
    "np": (0, 4, "p", 9),
    "n1p": (1, 5, "p", 9),
    "n2p": (2, 6, "p", 9),
    "n3p": (3, 7, "p", 9),
}


def scope(name):
    return jax.named_scope(name) if PROF else contextlib.nullcontext()


def body(x_hbm, tbl_hbm, wt_hbm, cc_hbm, ckr_hbm, wq_hbm, wdkv_hbm, g_hbm, wuk_hbm, wuv_hbm, wo_hbm,
         y_v, pc_v, pk_v,
         x_v, tbl_v, wt_s, ckr_v, wq_v, wdkv_v, g_v, wuk_v, wuv_v, wo_v, ob_s,
         kc, nc, wukt, wuvt, q_s, qn_s, qr_s, s_s, p_s, a_s, o_s, m_s, l_s, bias_s,
         loc_sem, send_sem, recv_sem, diag_sem):
    me = lax.axis_index("pool")
    core = lax.rem(me, 2)
    cx = lax.rem(lax.div(me, 2), 2)
    cy = lax.div(me, 4)
    fp = 1 - 2 * core
    fx = 2 - 4 * cx
    fy = 4 - 8 * cy
    peer = {"p": me + fp, "x": me + fx, "y": me + fy, "d": me + fx + fy}

    barrier = pltpu.get_barrier_semaphore()
    for d in ("x", "y", "p"):
        pl.semaphore_signal(barrier, inc=1, device_id=(peer[d],), device_id_type=MESH)

    n_loc = [0]

    def local(src, dst):
        cp = pltpu.make_async_copy(src, dst, loc_sem.at[n_loc[0]])
        n_loc[0] += 1
        cp.start()
        return cp

    ld_kr = local(ckr_hbm.at[pl.ds(0, 4)], ckr_v)
    ld_c = [local(cc_hbm.at[pl.ds(128 * h, 128)], kc.at[0, h, pl.ds(0, 128)]) for h in range(2)]
    ld_tbl = local(tbl_hbm, tbl_v)
    ld_x = local(x_hbm, x_v)
    ld_dkv = local(wdkv_hbm, wdkv_v)
    ld_small = [local(wt_hbm, wt_s), local(g_hbm, g_v)]
    ld_uk = local(wuk_hbm, wuk_v)
    ld_q = [local(wq_hbm.at[:, pl.ds(g * GCOLS, GCOLS)], wq_v.at[g]) for g in range(NGROUP)]
    ld_uv = local(wuv_hbm, wuv_v)
    ld_o = local(wo_hbm, wo_v)

    lane = lax.broadcasted_iota(jnp.int32, (TOK, 128), 1)
    low = lane < RD

    ld_kr.wait()
    for h in range(2):
        kr = ckr_v[pl.ds(2 * h, 2)].reshape(128, RD)
        kc[0, h, pl.ds(128, 16), :] = jnp.concatenate([kr[16 * u:16 * u + 16] for u in range(8)], axis=-1)

    def half_of(c, h):
        return kc.at[c] if h is None else kc.at[c, h]

    def flow(name):
        if name in FLOWS:
            sc, sh, tc, th, d = FLOWS[name]
            src, dst, s_sem, r_sem = half_of(sc, sh), half_of(tc, th), send_sem.at[0], recv_sem.at[tc]
        else:
            ss, ts, d, r = NEWS[name]
            src, dst, s_sem, r_sem = nc.at[ss], nc.at[ts], send_sem.at[1], recv_sem.at[r]
        return pltpu.make_async_remote_copy(src_ref=src, dst_ref=dst, send_sem=s_sem, recv_sem=r_sem,
                                            device_id=(peer[d],), device_id_type=MESH)

    def sends(*names):
        for name in names:
            flow(name).start()

    def arrive(c):
        with scope(f"wait_c{c}"):
            pltpu.make_async_copy(kc.at[c], kc.at[c], recv_sem.at[c]).wait()

    def arrive_new(r):
        first, n = {8: (1, 3), 9: (4, 4)}[r]
        with scope(f"wait_n{r}"):
            pltpu.make_async_copy(nc.at[pl.ds(first, n)], nc.at[pl.ds(first, n)], recv_sem.at[r]).wait()

    with scope("tables"):
        ld_tbl.wait()
        k_lane = lax.rem(lane, 32)
        freq = jnp.zeros((TOK, 128), F32)
        for k, f in enumerate(INV_FREQ):
            freq = jnp.where(k_lane == k, f, freq)
        n_pages = jnp.sum(jnp.where(tbl_v[0:1] >= 0, 1.0, 0.0), axis=-1, keepdims=True)
        pos = lax.broadcasted_iota(jnp.int32, (TOK, 128), 0).astype(F32) + jnp.broadcast_to(n_pages * TOK, (TOK, 128))
        ang = pos * freq
        cos_t = jnp.cos(ang)
        sin_t = jnp.sin(ang)
        sin_t = jnp.where(lax.rem(lane, 64) < 32, -sin_t, sin_t)

    def rope2(v64):
        v = jnp.concatenate([v64, v64], axis=-1)
        return v * cos_t + pltpu.roll(v, 32, 1) * sin_t

    with scope("barrier"):
        pl.semaphore_wait(barrier, 3)
    pl.semaphore_signal(diag_sem, inc=1, device_id=(peer["x"],), device_id_type=MESH)
    with scope("send0"):
        for cp in ld_c:
            cp.wait()
        sends("x0", "y1", "p0", "x1", "y0")

    with scope("mult"):
        tbl = tbl_v[...]
        ids = (tbl[0:1] * 4 + tbl[1:2]).astype(F32)
        ids_col = jnp.transpose(jnp.broadcast_to(ids, (128, 256)))
        seg = lax.div(lax.broadcasted_iota(jnp.int32, (1, 256), 1), 64)
        flips = {0: 0, 1: fp, 2: fx, 4: fy, 3: fp + fx, 5: fp + fy, 6: fx + fy, 7: fp + fx + fy}
        for c, ((ra, ha), (rb, hb)) in enumerate(CHUNKS):
            pa = (me + flips[ra]) * 4 + 2 * ha
            pb = (me + flips[rb]) * 4 + 2 * hb
            want = jnp.where(seg == 0, pa, jnp.where(seg == 1, pa + 1, jnp.where(seg == 2, pb, pb + 1))).astype(F32)
            parts = []
            for t in range(2):
                hit = jnp.where(ids_col == want[:, t * 128:(t + 1) * 128], 1.0, 0.0)
                parts.append(jnp.sum(hit, axis=0, keepdims=True))
            cnt = jnp.concatenate(parts, axis=-1)
            bias_s[c] = jnp.where(cnt > 0.0, jnp.log2(jnp.maximum(cnt, 1.0)), -jnp.inf)

    with scope("newlat"):
        ld_x.wait()
        ld_dkv.wait()
        for cp in ld_small:
            cp.wait()
        kv = lax.dot_general(x_v[...], wdkv_v[...], (((1,), (1,)), ((), ())), preferred_element_type=F32)
        latp = kv[:, :LAT]
        inv_rms = lax.rsqrt(jnp.mean(latp * latp, axis=-1, keepdims=True) + EPS)
        nc[0, pl.ds(0, TOK), :] = (latp * inv_rms * g_v[...].astype(F32).reshape(1, LAT)).astype(BF)
        kr_dup = rope2(kv[:, LAT:])
        kr_low = jnp.where(low, kr_dup, 0.0).astype(BF)
        for u in range(2):
            pair = jnp.where(low[:16], kr_dup[32 * u:32 * u + 16], kr_dup[32 * u + 16:32 * u + 32])
            nc[0, pl.ds(TOK, 16), pl.ds(128 * u, 128)] = pair.astype(BF)
        nc[0, pl.ds(TOK, 16), pl.ds(256, 256)] = jnp.full((16, 256), wt_s[0, 0], jnp.int32).astype(F32).astype(BF)

    r_i = lax.broadcasted_iota(jnp.int32, (256, 256), 0)
    c_i = lax.broadcasted_iota(jnp.int32, (256, 256), 1)
    perm = (r_i == lax.rem(c_i, 16) * 16 + lax.div(c_i, 16)).astype(F32).astype(BF)

    def reorder(src, dst):
        for blk in range(0, 32, 2):
            rows = jnp.concatenate([src[pl.ds((blk + v) * 256, 256), :] for v in range(2)], axis=-1)
            t = jnp.dot(perm, rows, preferred_element_type=F32).astype(BF)
            for v in range(2):
                dst[:, pl.ds((blk + v) * 16, 16), :] = t[:, v * 128:(v + 1) * 128].reshape(NH, 16, 128)

    with scope("reorder_uk"):
        ld_uk.wait()
        reorder(wuk_v, wukt)

    def lift(g):
        for k in range(GROUP):
            h = g * GROUP + k
            q_s[pl.ds(h * TOK, TOK), :] = lax.dot_general(
                qn_s[h], wukt[h], (((1,), (1,)), ((), ())), preferred_element_type=F32).astype(BF)

    for g in range(NGROUP):
        with scope(f"waitq{g}"):
            ld_q[g].wait()
        with scope(f"query{g}"):
            qg = jnp.dot(x_v[...], wq_v[g], preferred_element_type=F32).astype(BF).astype(F32)
            if g:
                lift(g - 1)
            for k in range(GROUP):
                h = g * GROUP + k
                qn_s[h] = qg[:, k * HQ:k * HQ + ND].astype(BF)
                qr_s[pl.ds(h * TOK, TOK), :] = rope2(qg[:, k * HQ + ND:(k + 1) * HQ]).astype(BF)

    NT = (((1,), (1,)), ((), ()))
    row_tok = lax.rem(lax.broadcasted_iota(jnp.int32, (BLK, TOK), 0), TOK)
    causal = lax.broadcasted_iota(jnp.int32, (BLK, TOK), 1) <= row_tok
    lane16 = lax.broadcasted_iota(jnp.int32, (16, 128), 1) < RD

    def rope_keys(c):
        if c < 0:
            return kr_low
        out = []
        for h in range(2):
            for u in range(4):
                t = kc[c, h, pl.ds(128, 16), pl.ds(128 * u, 128)].astype(F32)
                out += [jnp.where(lane16, t, 0.0), jnp.where(lane16, 0.0, t)]
        return jnp.concatenate(out, axis=0).astype(BF)

    def keys_of(c):
        if c < 0:
            return nc[0, pl.ds(0, TOK), :]
        return jnp.concatenate([kc[c, h, pl.ds(0, 128), :] for h in range(2)], axis=0)

    def scores(c, b, slot, kbd):
        rows = pl.ds(b * BLK, BLK)
        s = lax.dot_general(q_s[rows, :], keys_of(c), NT, preferred_element_type=F32)
        s = s + lax.dot_general(qr_s[rows, :], kbd, NT, preferred_element_type=F32)
        if c < 0:
            s_s[slot, :, :TOK] = s
        else:
            s_s[slot] = s

    def weigh(c, b, slot):
        rows = pl.ds(b * BLK, BLK)
        if c < 0:
            t = jnp.where(causal, s_s[slot, :, :TOK] * SCALE2, -jnp.inf)
            mx = jnp.max(t, axis=-1, keepdims=True)
            p = jnp.exp2(t - mx)
            m_s[rows, :] = jnp.broadcast_to(mx, (BLK, 128))
            l_s[rows, :] = jnp.concatenate([p, jnp.zeros_like(p)], axis=-1)
            p_s[slot, :, :TOK] = p.astype(BF)
            return
        t = s_s[slot] * SCALE2 + bias_s[c]
        mx = jnp.max(jnp.maximum(t[:, :128], t[:, 128:]), axis=-1, keepdims=True)
        m_old = m_s[rows, :]
        m_new = jnp.maximum(m_old, jnp.broadcast_to(mx, (BLK, 128)))
        alpha = jnp.exp2(m_old - m_new)
        p = jnp.exp2(t - jnp.concatenate([m_new, m_new], axis=-1))
        m_s[rows, :] = m_new
        a_s[slot] = alpha
        l_s[rows, :] = l_s[rows, :] * alpha + (p[:, :128] + p[:, 128:])
        p_s[slot] = p.astype(BF)

    def combine(c, b, slot):
        rows = pl.ds(b * BLK, BLK)
        if c < 0:
            o_s[rows, :] = jnp.dot(p_s[slot, :, :TOK], keys_of(c), preferred_element_type=F32)
            return
        a4 = jnp.concatenate([a_s[slot]] * 4, axis=-1)
        o_s[rows, :] = o_s[rows, :] * a4 + jnp.dot(p_s[slot], keys_of(c), preferred_element_type=F32)

    def before(c):
        if c == -1:
            arrive(2)
            sends("dy", "dx", "p2", "nx", "ny", "np")
            pl.semaphore_wait(diag_sem, 1)
            sends("nd")
        elif c == 1:
            arrive(1)
        elif c == 3:
            arrive(3)
        elif c == 4:
            arrive(4)
            sends("p4")
        elif c == 5:
            arrive(5)
        elif c == 6:
            arrive(6)
            sends("p6")
        elif c == 7:
            with scope("reorder_uv"):
                ld_uv.wait()
                reorder(wuv_v, wuvt)
            arrive(7)

    seq = [(c, b) for c in (-1, 0, 1, 2, 4, 3, 5, 6, 7) for b in range(ROWS // BLK)]
    for n in range(len(seq) + 2):
        if n < len(seq) and seq[n][1] == 0:
            before(seq[n][0])
            kbd = rope_keys(seq[n][0])
        with scope(f"attend{seq[n][0] if n < len(seq) else 99}"):
            if n < len(seq):
                scores(*seq[n], n % 2, kbd)
            if n == 0:
                lift(NGROUP - 1)
            if n >= 2:
                combine(*seq[n - 2], n % 2)
            if 1 <= n <= len(seq):
                weigh(*seq[n - 1], (n - 1) % 2)

    with scope("values"):
        for h in range(NH):
            rows = pl.ds(h * TOK, TOK)
            denom = jnp.sum(l_s[rows, :], axis=-1, keepdims=True)
            ol = (o_s[rows, :] / denom).astype(BF)
            ob_s[:, pl.ds(h * ND, ND)] = jnp.dot(ol, wuvt[h], preferred_element_type=F32).astype(BF)

    arrive_new(8)
    sends("n1p", "n2p", "n3p")
    with scope("outproj"):
        ld_o.wait()
        for j in range(DM // NB):
            cols = pl.ds(j * NB, NB)
            acc = jnp.dot(ob_s[...], wo_v[:, cols], preferred_element_type=F32)
            y_v[:, cols] = (x_v[:, cols].astype(F32) + acc).astype(BF)

    arrive_new(9)
    with scope("page"):
        mine = me.astype(F32)
        page = jnp.zeros((TOK, LAT), F32)
        packed = jnp.zeros((16, 256), F32)
        for r in range(8):
            hit = nc[r, pl.ds(TOK, 16), pl.ds(256, 256)].astype(F32) == mine
            packed = jnp.where(hit, nc[r, pl.ds(TOK, 16), pl.ds(0, 256)].astype(F32), packed)
            hit = jnp.concatenate([jnp.concatenate([hit] * 2, axis=-1)] * 4, axis=0)
            page = jnp.where(hit, nc[r, pl.ds(0, TOK), :].astype(F32), page)
        pc_v[...] = page.astype(BF)
        packed = packed.astype(BF)
        for u in range(4):
            pk_v[pl.ds(16 * u, 16), :] = packed[:, RD * u:RD * (u + 1)]
    with scope("final_wait"):
        pltpu.make_async_copy(kc.at[pl.ds(0, 7)], kc.at[pl.ds(0, 7)], send_sem.at[0]).wait()
        pltpu.make_async_copy(nc.at[pl.ds(0, 7)], nc.at[pl.ds(0, 7)], send_sem.at[1]).wait()


def finish_body(y_v, cc_v, ckr_v, pc_v, pk_v, y_hbm, cco_hbm, ckro_hbm, sem):
    copies = [
        pltpu.make_async_copy(src, dst, sem.at[n]) for n, (src, dst) in enumerate([
            (y_v, y_hbm),
            (cc_v.at[pl.ds(0, 4)], cco_hbm.at[pl.ds(0, 4)]),
            (pc_v, cco_hbm.at[4]),
            (ckr_v.at[pl.ds(0, 4)], ckro_hbm.at[pl.ds(0, 4)]),
            (pk_v, ckro_hbm.at[4]),
        ])
    ]
    for cp in copies:
        cp.start()
    for cp in copies:
        cp.wait()


def finish(y, cc, ckr, pc, pk):
    return pl.pallas_call(
        finish_body,
        name="mla_finish",
        out_shape=(
            jax.ShapeDtypeStruct((TOK, DM), BF),
            jax.ShapeDtypeStruct((5, TOK, LAT), BF),
            jax.ShapeDtypeStruct((5, TOK, RD), BF),
        ),
        in_specs=[pl.BlockSpec(memory_space=pltpu.VMEM)] * 5,
        out_specs=(pl.BlockSpec(memory_space=pl.ANY),) * 3,
        scratch_shapes=[pltpu.SemaphoreType.DMA((5,))],
        compiler_params=pltpu.CompilerParams(vmem_limit_bytes=4 * 1024 * 1024),
    )(y, cc, ckr, pc, pk)


def fused(*args):
    dma = pltpu.SemaphoreType.DMA
    args = [pltpu.with_memory_space_constraint(a, pltpu.HBM) for a in args]
    return pl.pallas_call(
        body,
        name="mla_prefill",
        out_shape=(
            jax.ShapeDtypeStruct((TOK, DM), BF),
            jax.ShapeDtypeStruct((TOK, LAT), BF),
            jax.ShapeDtypeStruct((TOK, RD), BF),
        ),
        in_specs=[pl.BlockSpec(memory_space=pltpu.HBM)] * len(args),
        out_specs=(pl.BlockSpec(memory_space=pltpu.VMEM),) * 3,
        scratch_shapes=[
            pltpu.VMEM((TOK, DM), BF),
            pltpu.VMEM((2, 256), jnp.int32),
            pltpu.SMEM((1, 2), jnp.int32),
            pltpu.VMEM((4, TOK, RD), BF),
            pltpu.VMEM((NGROUP, DM, GCOLS), BF),
            pltpu.VMEM((LAT + RD, DM), BF),
            pltpu.VMEM((LAT,), BF),
            pltpu.VMEM((LAT * NH, ND), BF),
            pltpu.VMEM((LAT * NH, ND), BF),
            pltpu.VMEM((DM, DM), BF),
            pltpu.VMEM((TOK, DM), BF),
            pltpu.VMEM((8, 2, HALF, LAT), BF),
            pltpu.VMEM((8, NEWR, LAT), BF),
            pltpu.VMEM((NH, LAT, ND), BF),
            pltpu.VMEM((NH, LAT, ND), BF),
            pltpu.VMEM((ROWS, LAT), BF),
            pltpu.VMEM((NH, TOK, ND), BF),
            pltpu.VMEM((ROWS, 128), BF),
            pltpu.VMEM((2, BLK, 256), F32),
            pltpu.VMEM((2, BLK, 256), BF),
            pltpu.VMEM((2, BLK, 128), F32),
            pltpu.VMEM((ROWS, LAT), F32),
            pltpu.VMEM((ROWS, 128), F32),
            pltpu.VMEM((ROWS, 128), F32),
            pltpu.VMEM((8, 1, 256), F32),
            dma((15,)),
            dma((2,)),
            dma((10,)),
            pltpu.SemaphoreType.REGULAR,
        ],
        compiler_params=pltpu.CompilerParams(collective_id=0, has_side_effects=True, vmem_limit_bytes=50 * 1024 * 1024),
    )(*args)


def solution(mesh):
    def device_step(hidden, pre_len, pre_table, wr_table, cache_c, cache_kr, w_q, w_dkv, g_kv, w_uk, w_uv, w_o):
        y, pc, pk = fused(
            hidden.reshape(TOK, DM), pre_table.reshape(256, 2).T, wr_table.reshape(1, 2), cache_c.reshape(5 * TOK, LAT), cache_kr[0],
            w_q, w_dkv.T, g_kv, w_uk.reshape(LAT * NH, ND), w_uv.reshape(LAT * NH, ND), w_o)
        y, c_out, kr_out = finish(y, cache_c[0], cache_kr[0], pc, pk)
        return y[None], c_out[None], kr_out[None]

    row = P("pool")
    rep = P()
    return jax.shard_map(device_step, mesh=mesh, in_specs=(row,) * 6 + (rep,) * 6, out_specs=(row, row, row), check_vma=False)
```

time: 26.6 us -> 23 us (0.86)
  Pallas kernels: 25.6 us -> 22.1 us
    pallas_call x1, Pallas kernels: 23.3 us -> 21.2 us  [fused(): pl.pallas_call(body, name='mla_prefill', out_shape=(jax.ShapeDtypeStruct(...]
    pallas_call x1, Pallas kernels: 2.28 us -> 0.87 us  [finish(): pl.pallas_call(finish_body, name='mla_finish', out_shape=(jax.ShapeDtypeS...]
where the time goes in v4:
time: 23 us; the launch traced here: 22.9 us
  Pallas kernels  22.1 us (96%)
  between operations  0.83 us (4%)
    pallas_call x1, Pallas kernels, fused(): pl.pallas_call(body, name='mla_prefill', out_shape=(jax.ShapeDtypeStruct(...  21.2 us
    pallas_call x1, Pallas kernels, finish(): pl.pallas_call(finish_body, name='mla_finish', out_shape=(jax.ShapeDtypeS...  0.87 us

profile of v4, /device:TPU:0, one launch (start us, length us, event | category | flops | bytes accessed | tf_op | source)
XLA Modules:
  0.0 22.9 jit_solution(13218939011672894245)
XLA Ops:
  0.6 0.0 copy-start
  0.6 0.0 copy-start.1
  0.7 21.2 %mla_prefill.1 = (bf16[64,2048]{1,0:T(8,128)(2,1)S(1)}, bf16[64,512]{1,0:T(8,128)(2,1)S(1)}, bf16[64,64]{1,0:T(8,128)(2,1)S(1)}) custom-call(bf16[64,2048]{1,0:T(8,128)(2,1)} %bitcast.21, s32[2,256]{1,0:T(2,128)} %bitcast.22, s32[1,2]{1,0:T(1,128)} %bitcast.23, bf16[320,512]{1,0:T(8,128)(2,1)} %bitcast.14, bf16[5,64,64]{2,1,0:T(8,128)(2,1)} %bitcast.16, ...), custom_call_target="tpu_custom_call" | custom-call | tf_op jit(solution)/shard_map/mla_prefill/pallas_call | solution.py:403
  21.9 0.0 copy-done
  21.9 0.0 copy-done.1
  21.9 0.9 %mla_finish.1 = (bf16[64,2048]{1,0:T(8,128)(2,1)}, bf16[5,64,512]{2,1,0:T(8,128)(2,1)}, bf16[5,64,64]{2,1,0:T(8,128)(2,1)}) custom-call(bf16[64,2048]{1,0:T(8,128)(2,1)S(1)} %get-tuple-element.9.y_v, bf16[5,64,512]{2,1,0:T(8,128)(2,1)S(1)} %bitcast.15, bf16[5,64,64]{2,1,0:T(8,128)(2,1)S(1)} %bitcast.17, bf16[64,512]{1,0:T(8,128)(2,1)S(1)} %get-tuple-element.10.pc_v, ...), custom_call_target="tpu_custom_call" | custom-call | tf_op jit(solution)/shard_map/mla_finish/pallas_call | solution.py:385
Async XLA Ops:
  0.6 21.3 %copy-start = (bf16[1,5,64,512]{3,2,1,0:T(8,128)(2,1)S(1)}, bf16[1,5,64,512]{3,2,1,0:T(8,128)(2,1)}, u32[]{:S(2)}) copy-start(bf16[1,5,64,512]{3,2,1,0:T(8,128)(2,1)} %param.15) | copy-start | bytes 983044
  0.6 21.3 %copy-start.1 = (bf16[1,5,64,64]{3,2,1,0:T(8,128)(2,1)S(1)}, bf16[1,5,64,64]{3,2,1,0:T(8,128)(2,1)}, u32[]{:S(2)}) copy-start(bf16[1,5,64,64]{3,2,1,0:T(8,128)(2,1)} %param.16) | copy-start | bytes 122884

commit v5 on v4

--- a/solution.py
+++ b/solution.py
@@ -28,6 +28,7 @@
 NB = 512
 NGROUP = NH // GROUP
 BLK = 256
+NBLK = ROWS // BLK
 SCALE2 = float((ND + RD) ** -0.5 * math.log2(math.e))
 INV_FREQ = [float(np.float32(10000.0 ** (-k / 32.0))) for k in range(32)]
 
@@ -59,7 +60,7 @@
 NEWS = {
     "nx": (0, 1, "x", 8),
     "ny": (0, 2, "y", 8),
-    "nd": (0, 3, "d", 8),
+    "nd": (0, 3, "d", 10),
     "np": (0, 4, "p", 9),
     "n1p": (1, 5, "p", 9),
     "n2p": (2, 6, "p", 9),
@@ -73,8 +74,8 @@
 
 def body(x_hbm, tbl_hbm, wt_hbm, cc_hbm, ckr_hbm, wq_hbm, wdkv_hbm, g_hbm, wuk_hbm, wuv_hbm, wo_hbm,
          y_v, pc_v, pk_v,
-         x_v, tbl_v, wt_s, ckr_v, wq_v, wdkv_v, g_v, wuk_v, wuv_v, wo_v, ob_s,
-         kc, nc, wukt, wuvt, q_s, qn_s, qr_s, s_s, p_s, a_s, o_s, m_s, l_s, bias_s,
+         x_v, tbl_v, wt_s, ckr_v, wq_v, wdkv_v, g_v, wuk_v, wuv_v, wo_v, ob_s, y_acc,
+         kc, nc, wukt, wuvt, q_s, qraw_s, qn_s, qr_s, s_s, p_s, a_s, o_s, m_s, l_s, bias_s,
          loc_sem, send_sem, recv_sem, diag_sem):
     me = lax.axis_index("pool")
     core = lax.rem(me, 2)
@@ -100,7 +101,7 @@
     ld_kr = local(ckr_hbm.at[pl.ds(0, 4)], ckr_v)
     ld_c = [local(cc_hbm.at[pl.ds(128 * h, 128)], kc.at[0, h, pl.ds(0, 128)]) for h in range(2)]
     ld_tbl = local(tbl_hbm, tbl_v)
-    ld_x = local(x_hbm, x_v)
+    ld_x = local(x_hbm, x_v.at[pl.ds(0, TOK)])
     ld_dkv = local(wdkv_hbm, wdkv_v)
     ld_small = [local(wt_hbm, wt_s), local(g_hbm, g_v)]
     ld_uk = local(wuk_hbm, wuk_v)
@@ -108,6 +109,12 @@
     ld_uv = local(wuv_hbm, wuv_v)
     ld_o = local(wo_hbm, wo_v)
 
+    x_v[pl.ds(TOK, TOK), :] = jnp.zeros((TOK, DM), BF)
+    for b in range(NBLK):
+        ob_s[b, pl.ds(TOK, TOK), :] = jnp.zeros((TOK, GROUP * ND), BF)
+    for pr in range(NH // 2):
+        qn_s[pr, pl.ds(0, TOK), pl.ds(ND, ND)] = jnp.zeros((TOK, ND), BF)
+        qn_s[pr, pl.ds(TOK, TOK), pl.ds(0, ND)] = jnp.zeros((TOK, ND), BF)
     lane = lax.broadcasted_iota(jnp.int32, (TOK, 128), 1)
     low = lane < RD
 
@@ -138,7 +145,7 @@
             pltpu.make_async_copy(kc.at[c], kc.at[c], recv_sem.at[c]).wait()
 
     def arrive_new(r):
-        first, n = {8: (1, 3), 9: (4, 4)}[r]
+        first, n = {8: (1, 2), 10: (3, 1), 9: (4, 4)}[r]
         with scope(f"wait_n{r}"):
             pltpu.make_async_copy(nc.at[pl.ds(first, n)], nc.at[pl.ds(first, n)], recv_sem.at[r]).wait()
 
@@ -189,7 +196,7 @@
         ld_dkv.wait()
         for cp in ld_small:
             cp.wait()
-        kv = lax.dot_general(x_v[...], wdkv_v[...], (((1,), (1,)), ((), ())), preferred_element_type=F32)
+        kv = lax.dot_general(x_v[pl.ds(0, TOK), :], wdkv_v[...], (((1,), (1,)), ((), ())), preferred_element_type=F32)
         latp = kv[:, :LAT]
         inv_rms = lax.rsqrt(jnp.mean(latp * latp, axis=-1, keepdims=True) + EPS)
         nc[0, pl.ds(0, TOK), :] = (latp * inv_rms * g_v[...].astype(F32).reshape(1, LAT)).astype(BF)
@@ -209,29 +216,36 @@
             rows = jnp.concatenate([src[pl.ds((blk + v) * 256, 256), :] for v in range(2)], axis=-1)
             t = jnp.dot(perm, rows, preferred_element_type=F32).astype(BF)
             for v in range(2):
-                dst[:, pl.ds((blk + v) * 16, 16), :] = t[:, v * 128:(v + 1) * 128].reshape(NH, 16, 128)
+                for h in range(NH):
+                    dst[h // 2, pl.ds((blk + v) * 16, 16), pl.ds((h % 2) * ND, ND)] = t[16 * h:16 * h + 16, v * 128:(v + 1) * 128]
 
     with scope("reorder_uk"):
         ld_uk.wait()
         reorder(wuk_v, wukt)
 
     def lift(g):
+        for pr in range(g * GROUP // 2, (g + 1) * GROUP // 2):
+            q_s[pl.ds(pr * 2 * TOK, 2 * TOK), :] = lax.dot_general(
+                qn_s[pr], wukt[pr], (((1,), (1,)), ((), ())), preferred_element_type=F32).astype(BF)
+
+    def post(g):
+        qg = qraw_s[g % 2].astype(BF).astype(F32)
         for k in range(GROUP):
             h = g * GROUP + k
-            q_s[pl.ds(h * TOK, TOK), :] = lax.dot_general(
-                qn_s[h], wukt[h], (((1,), (1,)), ((), ())), preferred_element_type=F32).astype(BF)
+            qn_s[h // 2, pl.ds((h % 2) * TOK, TOK), pl.ds((h % 2) * ND, ND)] = qg[:, k * HQ:k * HQ + ND].astype(BF)
+            qr_s[pl.ds(h * TOK, TOK), :] = rope2(qg[:, k * HQ + ND:(k + 1) * HQ]).astype(BF)
 
     for g in range(NGROUP):
         with scope(f"waitq{g}"):
             ld_q[g].wait()
         with scope(f"query{g}"):
-            qg = jnp.dot(x_v[...], wq_v[g], preferred_element_type=F32).astype(BF).astype(F32)
+            qraw_s[g % 2] = jnp.dot(x_v[...], wq_v[g], preferred_element_type=F32)[:TOK]
             if g:
+                post(g - 1)
                 lift(g - 1)
-            for k in range(GROUP):
-                h = g * GROUP + k
-                qn_s[h] = qg[:, k * HQ:k * HQ + ND].astype(BF)
-                qr_s[pl.ds(h * TOK, TOK), :] = rope2(qg[:, k * HQ + ND:(k + 1) * HQ]).astype(BF)
+    with scope("reorder_uv"):
+        ld_uv.wait()
+        reorder(wuv_v, wuvt)
 
     NT = (((1,), (1,)), ((), ()))
     row_tok = lax.rem(lax.broadcasted_iota(jnp.int32, (BLK, TOK), 0), TOK)
@@ -291,6 +305,33 @@
         a4 = jnp.concatenate([a_s[slot]] * 4, axis=-1)
         o_s[rows, :] = o_s[rows, :] * a4 + jnp.dot(p_s[slot], keys_of(c), preferred_element_type=F32)
 
+    def values(b):
+        for pr in range(b * GROUP // 2, (b + 1) * GROUP // 2):
+            rows = pl.ds(pr * 2 * TOK, 2 * TOK)
+            denom = jnp.sum(l_s[rows, :], axis=-1, keepdims=True)
+            ol = (o_s[rows, :] / denom).astype(BF)
+            val = jnp.dot(ol, wuvt[pr], preferred_element_type=F32).astype(BF)
+            ob_s[b, pl.ds(0, TOK), pl.ds((pr * 2 - b * GROUP) * ND, ND)] = val[:TOK, :ND]
+            ob_s[b, pl.ds(0, TOK), pl.ds((pr * 2 - b * GROUP) * ND + ND, ND)] = val[TOK:, ND:]
+
+    def project(b):
+        deep = pl.ds(b * GROUP * ND, GROUP * ND)
+        for j in range(DM // NB):
+            cols = pl.ds(j * NB, NB)
+            part = jnp.dot(ob_s[b], wo_v[deep, cols], preferred_element_type=F32)[:TOK]
+            if b == 0:
+                y_acc[:, cols] = x_v[pl.ds(0, TOK), cols].astype(F32) + part
+            elif b < NBLK - 1:
+                y_acc[:, cols] = y_acc[:, cols] + part
+            else:
+                y_v[:, cols] = (y_acc[:, cols] + part).astype(BF)
+
+    def pass_on(which, r, *names):
+        @pl.when(core == which)
+        def _():
+            arrive_new(r)
+            sends(*names)
+
     def before(c):
         if c == -1:
             arrive(2)
@@ -310,41 +351,36 @@
             arrive(6)
             sends("p6")
         elif c == 7:
-            with scope("reorder_uv"):
-                ld_uv.wait()
-                reorder(wuv_v, wuvt)
             arrive(7)
-
-    seq = [(c, b) for c in (-1, 0, 1, 2, 4, 3, 5, 6, 7) for b in range(ROWS // BLK)]
-    for n in range(len(seq) + 2):
-        if n < len(seq) and seq[n][1] == 0:
+            pass_on(1, 8, "n1p", "n2p")
+
+    seq = [(c, b) for c in (-1, 0, 1, 2, 4, 3, 5, 6, 7) for b in range(NBLK)]
+    end = len(seq)
+    for n in range(end + 4):
+        if n < end and seq[n][1] == 0:
             before(seq[n][0])
             kbd = rope_keys(seq[n][0])
-        with scope(f"attend{seq[n][0] if n < len(seq) else 99}"):
-            if n < len(seq):
+        if n == end:
+            ld_o.wait()
+            pass_on(1, 10, "n3p")
+            pass_on(0, 8, "n1p", "n2p")
+        with scope(f"attend{seq[n][0] if n < end else 99}") if n < end else contextlib.nullcontext():
+            if n < end:
                 scores(*seq[n], n % 2, kbd)
             if n == 0:
+                post(NGROUP - 1)
                 lift(NGROUP - 1)
-            if n >= 2:
+            if 2 <= n < end + 2:
                 combine(*seq[n - 2], n % 2)
-            if 1 <= n <= len(seq):
+            if 1 <= n <= end:
                 weigh(*seq[n - 1], (n - 1) % 2)
-
-    with scope("values"):
-        for h in range(NH):
-            rows = pl.ds(h * TOK, TOK)
-            denom = jnp.sum(l_s[rows, :], axis=-1, keepdims=True)
-            ol = (o_s[rows, :] / denom).astype(BF)
-            ob_s[:, pl.ds(h * ND, ND)] = jnp.dot(ol, wuvt[h], preferred_element_type=F32).astype(BF)
-
-    arrive_new(8)
-    sends("n1p", "n2p", "n3p")
-    with scope("outproj"):
-        ld_o.wait()
-        for j in range(DM // NB):
-            cols = pl.ds(j * NB, NB)
-            acc = jnp.dot(ob_s[...], wo_v[:, cols], preferred_element_type=F32)
-            y_v[:, cols] = (x_v[:, cols].astype(F32) + acc).astype(BF)
+            if end - NBLK <= n - 3 < end:
+                values(seq[n - 3][1])
+            if end - NBLK <= n - 4 < end:
+                project(seq[n - 4][1])
+    pass_on(0, 10, "n3p")
+    with scope("tail"):
+        project(NBLK - 1)
 
     arrive_new(9)
     with scope("page"):
@@ -411,7 +447,7 @@
         in_specs=[pl.BlockSpec(memory_space=pltpu.HBM)] * len(args),
         out_specs=(pl.BlockSpec(memory_space=pltpu.VMEM),) * 3,
         scratch_shapes=[
-            pltpu.VMEM((TOK, DM), BF),
+            pltpu.VMEM((2 * TOK, DM), BF),
             pltpu.VMEM((2, 256), jnp.int32),
             pltpu.SMEM((1, 2), jnp.int32),
             pltpu.VMEM((4, TOK, RD), BF),
@@ -421,13 +457,15 @@
             pltpu.VMEM((LAT * NH, ND), BF),
             pltpu.VMEM((LAT * NH, ND), BF),
             pltpu.VMEM((DM, DM), BF),
-            pltpu.VMEM((TOK, DM), BF),
+            pltpu.VMEM((NBLK, 2 * TOK, GROUP * ND), BF),
+            pltpu.VMEM((TOK, DM), F32),
             pltpu.VMEM((8, 2, HALF, LAT), BF),
             pltpu.VMEM((8, NEWR, LAT), BF),
-            pltpu.VMEM((NH, LAT, ND), BF),
-            pltpu.VMEM((NH, LAT, ND), BF),
+            pltpu.VMEM((NH // 2, LAT, 2 * ND), BF),
+            pltpu.VMEM((NH // 2, LAT, 2 * ND), BF),
             pltpu.VMEM((ROWS, LAT), BF),
-            pltpu.VMEM((NH, TOK, ND), BF),
+            pltpu.VMEM((2, TOK, GCOLS), F32),
+            pltpu.VMEM((NH // 2, 2 * TOK, 2 * ND), BF),
             pltpu.VMEM((ROWS, 128), BF),
             pltpu.VMEM((2, BLK, 256), F32),
             pltpu.VMEM((2, BLK, 256), BF),
@@ -438,7 +476,7 @@
             pltpu.VMEM((8, 1, 256), F32),
             dma((15,)),
             dma((2,)),
-            dma((10,)),
+            dma((11,)),
             pltpu.SemaphoreType.REGULAR,
         ],
         compiler_params=pltpu.CompilerParams(collective_id=0, has_side_effects=True, vmem_limit_bytes=50 * 1024 * 1024),

time: 23 us -> 22.5 us (0.978)
  Pallas kernels: 22.1 us -> 21.6 us
    pallas_call x1, Pallas kernels: 21.2 us -> 20.7 us  [fused(): pl.pallas_call(body, name='mla_prefill', out_shape=(jax.ShapeDtypeStruct(...]
where the time goes in v5:
time: 22.5 us; the launch traced here: 22.4 us
  Pallas kernels  21.6 us (96%)
  between operations  0.83 us (4%)
    pallas_call x1, Pallas kernels, fused(): pl.pallas_call(body, name='mla_prefill', out_shape=(jax.ShapeDtypeStruct(...  20.7 us
    pallas_call x1, Pallas kernels, finish(): pl.pallas_call(finish_body, name='mla_finish', out_shape=(jax.ShapeDtypeS...  0.87 us

profile of v5, /device:TPU:0, one launch (start us, length us, event | category | flops | bytes accessed | tf_op | source)
XLA Modules:
  0.0 22.4 jit_solution(13724782461430395573)
XLA Ops:
  0.6 0.0 copy-start
  0.6 0.0 copy-start.1
  0.7 20.7 %mla_prefill.1 = (bf16[64,2048]{1,0:T(8,128)(2,1)S(1)}, bf16[64,512]{1,0:T(8,128)(2,1)S(1)}, bf16[64,64]{1,0:T(8,128)(2,1)S(1)}) custom-call(bf16[64,2048]{1,0:T(8,128)(2,1)} %bitcast.21, s32[2,256]{1,0:T(2,128)} %bitcast.22, s32[1,2]{1,0:T(1,128)} %bitcast.23, bf16[320,512]{1,0:T(8,128)(2,1)} %bitcast.14, bf16[5,64,64]{2,1,0:T(8,128)(2,1)} %bitcast.16, ...), custom_call_target="tpu_custom_call" | custom-call | tf_op jit(solution)/shard_map/mla_prefill/pallas_call | solution.py:439
  21.4 0.0 copy-done
  21.4 0.0 copy-done.1
  21.4 0.9 %mla_finish.1 = (bf16[64,2048]{1,0:T(8,128)(2,1)}, bf16[5,64,512]{2,1,0:T(8,128)(2,1)}, bf16[5,64,64]{2,1,0:T(8,128)(2,1)}) custom-call(bf16[64,2048]{1,0:T(8,128)(2,1)S(1)} %get-tuple-element.9.y_v, bf16[5,64,512]{2,1,0:T(8,128)(2,1)S(1)} %bitcast.15, bf16[5,64,64]{2,1,0:T(8,128)(2,1)S(1)} %bitcast.17, bf16[64,512]{1,0:T(8,128)(2,1)S(1)} %get-tuple-element.10.pc_v, ...), custom_call_target="tpu_custom_call" | custom-call | tf_op jit(solution)/shard_map/mla_finish/pallas_call | solution.py:421
Async XLA Ops:
  0.6 20.8 %copy-start = (bf16[1,5,64,512]{3,2,1,0:T(8,128)(2,1)S(1)}, bf16[1,5,64,512]{3,2,1,0:T(8,128)(2,1)}, u32[]{:S(2)}) copy-start(bf16[1,5,64,512]{3,2,1,0:T(8,128)(2,1)} %param.15) | copy-start | bytes 983044
  0.6 20.8 %copy-start.1 = (bf16[1,5,64,64]{3,2,1,0:T(8,128)(2,1)S(1)}, bf16[1,5,64,64]{3,2,1,0:T(8,128)(2,1)}, u32[]{:S(2)}) copy-start(bf16[1,5,64,64]{3,2,1,0:T(8,128)(2,1)} %param.16) | copy-start | bytes 122884
